TPU v7x, 32 devices: a whole 2x2x4 slice. The times are simulated.
32 devices in a mesh: section: 2 (over y), expert: 2 (over x), tensor: 8 (over z, core).
Axes of the slice: x: 2, y: 2, z: 4, core: 2. Of those that a mesh axis runs over, the one named last changes fastest.
Arguments:
- query: bfloat16 [2, 512, 4096], P('expert', 'tensor', 'section'), may hold values from -24 to 24
- keys: bfloat16 [2, 512, 1024], P('expert', 'tensor', 'section'), may hold values from -24 to 24
- values: bfloat16 [2, 512, 1024], P('expert', 'tensor', 'section'), may hold values from -6 to 6
- residual: bfloat16 [2, 512, 4096], P('expert', 'tensor', 'section'), may hold values from -6 to 6
- routes: int32 [2, 512, 2], P('expert', 'tensor'), may hold values from 0 to 7, all different within a row; in each aligned block of 64 rows (0 to 63, 64 to 127, ..., all dimensions but the last counted through in order) at most 17 rows name the same one
- gates: float32 [2, 512, 2], P('expert', 'tensor'), may hold values from 0.1 to 0.9
- w_gate: bfloat16 [8, 4096, 8192], P('expert', None, 'tensor'), may hold values from -0.09375 to 0.09375
- w_up: bfloat16 [8, 4096, 8192], P('expert', None, 'tensor'), may hold values from -0.09375 to 0.09375
- w_down: bfloat16 [8, 8192, 4096], P('expert', 'tensor'), may hold values from -0.0625 to 0.0625
Outputs:
- layer_out: bfloat16 [2, 512, 4096], P('expert', 'tensor', 'section')
Inputs may be any that keep to these rules, and one draw needn't show every extreme that they name: `routes`: the 2 entries of a row differ. In the rows of one index of expert and tensor (aligned blocks of 64 positions, taken in order over sequences and positions) no expert is named more than 17 times.
All inputs are finite; a program needn't handle non-finite values.
Results may differ from a plain program's by a relative error of at most 0.014.
Values may be sent and summed in bfloat16 or wider, within the bound.
No kernel may reach another device: no remote copies, remote signals or barrier semaphores. Data moves between devices by JAX's collectives and lax.ppermute only.
A program may use at most 192 MiB of HBM per device.

v0:
```python
import math

import jax
import jax.numpy as jnp
from jax import lax
from jax.sharding import PartitionSpec as P

HD = 128
EXPERTS = 8
TOP = 2
HALF_CAP = 9


def from_partner(value, axis, stride):
    mask = 2**stride
    pairs = [(source, source ^ mask) for source in range(lax.axis_size(axis))]
    return lax.ppermute(value, axis, pairs)


def slot_table(picked, first_slot, slot_count):
    flattened = picked.reshape(-1)
    onehot = (flattened[:, None] == jnp.arange(EXPERTS)[None, :]).astype(jnp.int32)
    before = jnp.cumsum(onehot, axis=0) - onehot
    slot_index = jnp.sum(before * onehot, axis=1)
    target = slot_index * EXPERTS + flattened
    rows_wanted = first_slot * EXPERTS + jnp.arange(slot_count * EXPERTS)
    return rows_wanted[:, None] == target[None, :]


def pack_rows(token_rows, picked, first_slot, slot_count):
    slot_hits = slot_table(picked, first_slot, slot_count)
    token_count = token_rows.shape[0]
    single = jnp.any(slot_hits.reshape(slot_count * EXPERTS, token_count, TOP), axis=2).astype(
        jnp.bfloat16
    )
    packed = jnp.dot(single, token_rows, preferred_element_type=jnp.float32).astype(jnp.bfloat16)
    return packed.reshape(slot_count, EXPERTS, token_rows.shape[1])


def expert_inner(piece_rows, gate_cols, up_cols):
    gate_part = jnp.einsum(
        "red,edf->ref", piece_rows, gate_cols, preferred_element_type=jnp.float32
    )
    up_part = jnp.einsum("red,edf->ref", piece_rows, up_cols, preferred_element_type=jnp.float32)
    return (jax.nn.silu(gate_part) * up_part).astype(jnp.bfloat16)


def on_device(query, keys, values, residual, routes, gates, w_gate, w_up, w_down):
    key_all, value_all = (
        lax.all_gather(keys, "tensor", axis=1, tiled=True),
        lax.all_gather(values, "tensor", axis=1, tiled=True),
    )
    token_count = query.shape[1]
    length = key_all.shape[1]
    half_width = query.shape[2]
    local_heads = half_width // HD
    local_kv = keys.shape[2] // HD
    groups = local_heads // local_kv
    section_id = lax.axis_index("section")
    queries = query[0].reshape(token_count, local_kv, groups, HD)
    key_heads = key_all[0].reshape(length, local_kv, HD)
    value_heads = value_all[0].reshape(length, local_kv, HD)
    scores = jnp.einsum(
        "qkgd,tkd->kgqt", queries, key_heads, preferred_element_type=jnp.float32
    ) / math.sqrt(HD)
    start_row = lax.axis_index("tensor") * token_count
    query_positions = start_row + jnp.arange(token_count)
    causal = query_positions[:, None] >= jnp.arange(length)[None, :]
    masked = jnp.where(causal, scores, -1e30)
    row_peak = jnp.max(masked, axis=-1, keepdims=True)
    exp_terms = jnp.where(causal, jnp.exp(masked - row_peak), 0.0)
    weights = (exp_terms / jnp.sum(exp_terms, axis=-1, keepdims=True)).astype(jnp.bfloat16)
    context = jnp.einsum("kgqt,tkd->qkgd", weights, value_heads, preferred_element_type=jnp.float32)
    hidden_half = (
        residual[0].astype(jnp.float32) + context.reshape(token_count, half_width)
    ).astype(jnp.bfloat16)
    picked = routes[0]
    hidden = lax.all_gather(hidden_half, "section", axis=1, tiled=True)
    packed = pack_rows(hidden, picked, section_id * HALF_CAP, HALF_CAP)
    arrived = lax.all_to_all(packed, "expert", split_axis=1, concat_axis=0, tiled=True)
    inner_rows = expert_inner(lax.all_gather(arrived, "tensor", axis=0, tiled=True), w_gate, w_up)
    summed = lax.psum_scatter(
        jnp.einsum("ref,efd->red", inner_rows, w_down, preferred_element_type=jnp.float32).astype(
            jnp.bfloat16
        ),
        "tensor",
        scatter_dimension=0,
        tiled=True,
    )
    returned = lax.all_to_all(summed, "expert", split_axis=0, concat_axis=1, tiled=True)
    own_cols = lax.dynamic_slice_in_dim(returned, section_id * half_width, half_width, 2)
    other_cols = lax.dynamic_slice_in_dim(returned, (1 - section_id) * half_width, half_width, 2)
    partner_cols = from_partner(other_cols, "section", 0)
    first_half = jnp.where(section_id == 0, own_cols, partner_cols)
    second_half = jnp.where(section_id == 0, partner_cols, own_cols)
    returned_half = jnp.concatenate([first_half, second_half], axis=0)
    slot_total = returned_half.shape[0]
    slot_hits = slot_table(picked, 0, slot_total)
    weight_table = jnp.sum(
        slot_hits.astype(jnp.float32).reshape(slot_total * EXPERTS, token_count, TOP)
        * gates[0][None, :, :],
        axis=2,
    )
    expert_sum = jnp.einsum(
        "ct,cd->td",
        weight_table,
        returned_half.reshape(slot_total * EXPERTS, half_width).astype(jnp.float32),
        precision=lax.Precision.HIGHEST,
    )
    layer_out = (hidden_half.astype(jnp.float32) + expert_sum).astype(jnp.bfloat16)
    return layer_out[None]


def solution(mesh):
    return jax.shard_map(
        on_device,
        mesh=mesh,
        in_specs=(
            P("expert", "tensor", "section"),
            P("expert", "tensor", "section"),
            P("expert", "tensor", "section"),
            P("expert", "tensor", "section"),
            P("expert", "tensor", None),
            P("expert", "tensor", None),
            P("expert", None, "tensor"),
            P("expert", None, "tensor"),
            P("expert", "tensor", None),
        ),
        out_specs=P("expert", "tensor", "section"),
        check_vma=False,
    )
```

profile of v0, /device:TPU:0, one launch (start us, length us, event | category | flops | bytes accessed | tf_op | source)
XLA Modules:
  0.0 324.3 jit_solution(15335632785054796384)
XLA Ops:
  6.5 0.0 copy-start.1
  6.5 0.0 all-gather.2.cloned.1.call-start
  6.5 0.8 copy.79
  7.3 0.1 eq.25
  7.5 0.1 fusion.28
  7.6 0.2 reduce_window_sum.12
  7.8 0.2 select_reduce_fusion.1
  7.9 0.1 mul.48
  8.1 0.1 copy.80
  8.2 0.7 bitcast_add_fusion
  8.9 0.1 iota_compare_fusion.1
  9.0 16.7 %all_gather.12 = bf16[1,512,512]{2,1,0:T(8,128)(2,1)S(1)} all-gather(bf16[1,64,512]{2,1,0:T(8,128)(2,1)} %param.10), channel_id=1, replica_groups=mesh['section'=2,'expert'=2,'tensor'=8] {'tensor'}, dimensions={1}, use_global_device_ids=true | all-gather | bytes 589824 | tf_op jit(solution)/shard_map/all_gather | solution.py:50
  25.7 0.2 copy.73
  25.9 1.1 reshape_squeeze.14
  27.0 0.0 copy-done.1
  27.0 14.8 %all_gather.13 = bf16[1,512,512]{2,1,0:T(8,128)(2,1)S(1)} all-gather(bf16[1,64,512]{2,1,0:T(8,128)(2,1)S(1)} %copy-done.1), channel_id=1, replica_groups=mesh['section'=2,'expert'=2,'tensor'=8] {'tensor'}, dimensions={1}, use_global_device_ids=true | all-gather | bytes 589824 | tf_op jit(solution)/shard_map/all_gather | solution.py:51
  41.8 0.2 copy.76
  42.0 2.2 fusion.34
  44.2 0.0 copy-start
  44.2 2.1 convolution_bitcast_fusion
  46.4 0.3 copy.78
  46.7 0.2 reshape.53
  46.9 0.0 copy-done
  47.0 9.2 %all_gather.14 = bf16[64,4096]{1,0:T(8,128)(2,1)S(1)} all-gather(bf16[64,2048]{1,0:T(8,128)(2,1)S(1)} %fusion.21), channel_id=1, replica_groups=mesh['section'=2,'expert'=2,'tensor'=8] {'section'}, dimensions={1}, use_global_device_ids=true | all-gather | bytes 786432 | tf_op jit(solution)/shard_map/all_gather | solution.py:78
  56.2 0.1 compare_reduce_fusion
  56.3 0.4 fusion.2
  56.7 0.4 copy.81
  57.0 16.0 %all_to_all.36 = bf16[9,8,4096]{2,0,1:T(8,128)(2,1)S(1)} all-to-all(bf16[9,8,4096]{2,0,1:T(8,128)(2,1)S(1)} %copy.81), channel_id=1, replica_groups=mesh['section'=2,'expert'=2,'tensor'=8] {'expert'}, dimensions={1} | all-to-all | bytes 1179648 | tf_op jit(solution)/shard_map/all_to_all | solution.py:80
  73.0 1.3 copy.95
  74.3 0.0 all-gather.2.cloned.1.call-update
  74.4 0.2 all-reduce.3.cloned.1.call-start
  74.6 51.6 %all-gather.2.cloned.1.call-done = bf16[144,4,4096]{2,1,0:T(4,128)(2,1)} async-done(((bf16[18,4,4096]{2,1,0:T(4,128)(2,1)}), bf16[144,4,4096]{2,1,0:T(4,128)(2,1)}) %all-gather.2.cloned.1.call-update) | async-done | bytes 4718608 | tf_op jit(solution)/shard_map/all_gather | solution.py:81
  126.2 22.1 %fusion.3 = f32[4,144,1024]{2,1,0:T(8,128)S(1)} fusion(bf16[4,4096,1024]{2,1,0:T(8,128)(2,1)} %param.16, bf16[144,4,4096]{2,1,0:T(4,128)(2,1)} %all-gather.2.cloned.1.call-done), kind=kOutput, calls=%fused_computation.5 | convolution fusion | flops 4831838208 | bytes 40632320 | tf_op jit(solution)/shard_map/red,edf->ref/dot_general | solution.py:44
  148.3 31.9 %fusion.1 = bf16[144,4,4096]{2,0,1:T(8,128)(2,1)} fusion(bf16[4,1024,4096]{2,1,0:T(8,128)(2,1)} %param.17, f32[4,144,1024]{2,1,0:T(8,128)S(1)} %fusion.3, bf16[4,4096,1024]{2,1,0:T(8,128)(2,1)} %param.15, bf16[144,4,4096]{2,1,0:T(4,128)(2,1)} %all-gather.2.cloned.1.call-done), kind=kOutput, calls=%fused_computation.2 | convolution fusion | flops 9669574656 | bytes 78905344 | tf_op jit(solution)/shard_map/ref,efd->red/dot_general | solution.py:83
  180.1 8.2 %copy.86 = bf16[144,4,4096]{2,1,0:T(4,128)(2,1)} copy(bf16[144,4,4096]{2,0,1:T(8,128)(2,1)} %fusion.1) | data formatting | bytes 9437184 | tf_op jit(solution)/shard_map/convert_element_type | solution.py:83
  188.4 0.0 copy-start.3
  188.4 0.0 all-reduce.3.cloned.1.call-update
  188.4 0.6 copy-done.3
  189.0 0.6 dynamic-slice
  190.2 103.4 %all-reduce.3.cloned.1.call-done = bf16[144,4,4096]{2,1,0:T(4,128)(2,1)} async-done(((bf16[144,4,4096]{2,1,0:T(4,128)(2,1)}), bf16[144,4,4096]{2,1,0:T(4,128)(2,1)}) %all-reduce.3.cloned.1.call-update) | async-done | bytes 4718608
  293.7 2.1 constant_dynamic-slice_fusion
  295.8 0.0 copy-start.2
  295.8 3.6 %all-to-all-start.1 = ((bf16[18,4,4096]{2,1,0:T(4,128)(2,1)}), bf16[18,4,4096]{2,1,0:T(4,128)(2,1)S(1)}, u32[]{:S(2)}, u32[]{:S(2)}) async-start(bf16[18,4,4096]{2,1,0:T(4,128)(2,1)} %constant_dynamic-slice_fusion), calls=%async_computation.1 | async-start | bytes 1179648 | tf_op jit(solution)/shard_map/all_to_all | solution.py:90
  299.5 8.7 %all-to-all-done.1 = bf16[18,4,4096]{2,1,0:T(4,128)(2,1)S(1)} async-done(((bf16[18,4,4096]{2,1,0:T(4,128)(2,1)}), bf16[18,4,4096]{2,1,0:T(4,128)(2,1)S(1)}, u32[]{:S(2)}, u32[]{:S(2)}) %all-to-all-start.1) | async-done | bytes 589856 | tf_op jit(solution)/shard_map/all_to_all | solution.py:90
  308.1 0.3 copy.87
  308.4 0.1 all_to_all.33
  308.6 1.5 collective-permute-start
  310.1 0.0 copy-done.2
  310.1 0.1 select_reduce_fusion
  310.2 6.1 %collective-permute-done = bf16[9,8,2048]{2,1,0:T(8,128)(2,1)S(1)} collective-permute-done((bf16[9,8,2048]{2,1,0:T(8,128)(2,1)S(1)}, bf16[9,8,2048]{2,1,0:T(8,128)(2,1)S(1)}, u32[]{:S(2)}, u32[]{:S(2)}) %collective-permute-start) | collective-permute-done | bytes 294944 | tf_op jit(solution)/shard_map/ppermute | solution.py:17
  316.3 0.1 broadcast_select_fusion.1
  316.4 1.1 fusion.12
  (5 shorter events, 0.1 us)
Async XLA Ops:
  6.5 20.5 %copy-start.1 = (bf16[1,64,512]{2,1,0:T(8,128)(2,1)S(1)}, bf16[1,64,512]{2,1,0:T(8,128)(2,1)}, u32[]{:S(2)}) copy-start(bf16[1,64,512]{2,1,0:T(8,128)(2,1)} %param.11) | copy-start | bytes 196612
  6.5 119.7 %all-gather.2.cloned.1.call-start = ((), (), s32[]{:S(2)}) async-start(), calls=%async_computation.2 | async-start | bytes 5308416 | tf_op jit(solution)/shard_map/all_gather | solution.py:81
  44.2 2.7 copy-start
  74.4 219.3 %all-reduce.3.cloned.1.call-start = ((), (), s32[]{:S(2)}) async-start(), calls=%async_computation.3 | async-start | bytes 9437184
  188.4 0.7 copy-start.3
  295.8 14.3 %copy-start.2 = (f32[1,64,2]{1,2,0:T(2,128)S(1)}, f32[1,64,2]{1,2,0:T(2,128)}, u32[]{:S(2)}) copy-start(f32[1,64,2]{1,2,0:T(2,128)} %param.14) | copy-start | bytes 1540
  295.8 12.3 %all-to-all-start.1 = ((bf16[18,4,4096]{2,1,0:T(4,128)(2,1)}), bf16[18,4,4096]{2,1,0:T(4,128)(2,1)S(1)}, u32[]{:S(2)}, u32[]{:S(2)}) async-start(bf16[18,4,4096]{2,1,0:T(4,128)(2,1)} %constant_dynamic-slice_fusion), calls=%async_computation.1 | async-start | bytes 1179648 | tf_op jit(solution)/shard_map/all_to_all | solution.py:90
  308.6 7.7 %collective-permute-start = (bf16[9,8,2048]{2,1,0:T(8,128)(2,1)S(1)}, bf16[9,8,2048]{2,1,0:T(8,128)(2,1)S(1)}, u32[]{:S(2)}, u32[]{:S(2)}) collective-permute-start(bf16[9,8,2048]{2,1,0:T(8,128)(2,1)S(1)} %constant_dynamic-slice_fusion.1), channel_id=1, source_target_pairs={{0,16},{16,0},{1,17},{17,1},{2,18},{18,2},{3,19},{19,3},{4,20},{20... | collective-permute-start | bytes 884744 | tf_op jit(solution)/shard_map/ppermute | solution.py:17
Sparse Core Ops, SparseCore 0:
  74.5 51.6 all-gather.1
  188.5 105.1 all-reduce.2
where the time goes:
time: 325 us; the launch traced here: 324 us
  waiting for transfers between devices  170 us (52%)
  matrix products  59.8 us (18%)
  blocking collectives  56.7 us (17%)
  local copies, waits for them, and re-layouts  16.9 us (5%)
  between operations  14.2 us (4%)
  starting transfers between devices  5.4 us (2%)
    unnamed x3, waiting for transfers between devices  103 us
    all_gather x1, waiting for transfers between devices, on_device(): lax.all_gather(arrived, 'tensor', axis=0, tiled=True)  51.6 us
    dot_general x1, matrix products, on_device(): jnp.einsum('ref,efd->red', inner_rows, w_down, preferred_element_type=jnp...  31.9 us
    dot_general x1, matrix products, expert_inner(): jnp.einsum('red,edf->ref', piece_rows, up_cols, preferred_element_type=jn...  22.1 us
    all_gather x1, blocking collectives, on_device(): lax.all_gather(keys, 'tensor', axis=1, tiled=True)  16.7 us
    all_to_all x1, blocking collectives, on_device(): lax.all_to_all(packed, 'expert', split_axis=1, concat_axis=0, tiled=True)  16 us
    all_gather x1, blocking collectives, on_device(): lax.all_gather(values, 'tensor', axis=1, tiled=True)  14.8 us
    all_gather x1, blocking collectives, on_device(): hidden = lax.all_gather(hidden_half, 'section', axis=1, tiled=True)  9.22 us
  transfers between devices with their start and end apart: 4, of which 4 were waited for; matrix products, arithmetic and copies ran while one was open for 0% of the time, Pallas kernels for 0%

commit v1 on v0

v1 whole, which is shorter than its diff:
```python
import functools
import math

import jax
import jax.numpy as jnp
from jax import lax
from jax.experimental import pallas as pl
from jax.experimental.pallas import tpu as pltpu
from jax.sharding import PartitionSpec as P

HD = 128
EXPERTS = 8
TOP = 2
CAP = 17
META = 128
BF = jnp.bfloat16
F32 = jnp.float32


def swap(value, axis, mask):
    pairs = [(i, i ^ mask) for i in range(lax.axis_size(axis))]
    return lax.ppermute(value, axis, pairs)


def bits_of(axis, lowest):
    count = lax.axis_size(axis).bit_length() - 1
    return [(axis, 1 << b) for b in reversed(range(lowest, count))]


def gather_steps():
    return bits_of("tensor", 1) + bits_of("expert", 0) + [("tensor", 1)]


def gather_all(block, steps):
    for axis, mask in steps:
        block = jnp.concatenate([block, swap(block, axis, mask)], axis=0)
    return block


def scatter_sum(total, steps):
    for axis, mask in reversed(steps):
        half = total.shape[0] // 2
        arrived = swap(total[half:], axis, mask)
        total = (total[:half].astype(F32) + arrived.astype(F32)).astype(BF)
    return total


def hot_rows(rank_row, first, count):
    slots = lax.broadcasted_iota(jnp.int32, (count, rank_row.shape[1]), 0) + first
    return slots == rank_row


def inner_kernel(
    scal, x_own, x_oth, rank, wg_own, wg_oth, wu_own, wu_oth, out, rows_own, rows_oth, *, main, cap
):
    e, n = pl.program_id(0), pl.program_id(1)
    rank_row = rank[pl.ds(e, 1), :]

    def part(first, count):
        @pl.when(n == 0)
        def _():
            hot = hot_rows(rank_row, first, count).astype(BF)
            for src, dst in ((x_own, rows_own), (x_oth, rows_oth)):
                dst[first : first + count, :] = jnp.dot(
                    hot, src[...], preferred_element_type=F32
                ).astype(BF)

        mine = rows_own[first : first + count, :]
        rest = rows_oth[first : first + count, :]
        gate = jnp.dot(mine, wg_own[0], preferred_element_type=F32) + jnp.dot(
            rest, wg_oth[0], preferred_element_type=F32
        )
        up = jnp.dot(mine, wu_own[0], preferred_element_type=F32) + jnp.dot(
            rest, wu_oth[0], preferred_element_type=F32
        )
        out[0, first : first + count, :] = (gate / (1.0 + jnp.exp(-gate)) * up).astype(BF)

    part(0, main)
    if cap > main:

        @pl.when(scal[1 + e] > main)
        def _():
            part(main, cap - main)


def expert_inner(scal, x_own, x_oth, rank, w_gate, w_up, main, cap):
    experts, width, hidden = w_gate.shape
    half, tokens = width // 2, x_oth.shape[0]
    block = min(256, hidden)
    own = pl.BlockSpec((1, half, block), lambda e, n, s: (e, s[0], n))
    oth = pl.BlockSpec((1, half, block), lambda e, n, s: (e, 1 - s[0], n))
    return pl.pallas_call(
        functools.partial(inner_kernel, main=main, cap=cap),
        grid_spec=pltpu.PrefetchScalarGridSpec(
            num_scalar_prefetch=1,
            grid=(experts, hidden // block),
            in_specs=[
                pl.BlockSpec((tokens, half), lambda e, n, s: (0, 0)),
                pl.BlockSpec((tokens, half), lambda e, n, s: (0, 0)),
                pl.BlockSpec((experts, tokens), lambda e, n, s: (0, 0)),
                own,
                oth,
                own,
                oth,
            ],
            out_specs=pl.BlockSpec((1, cap, block), lambda e, n, s: (e, 0, n)),
            scratch_shapes=[pltpu.VMEM((cap, half), BF), pltpu.VMEM((cap, half), BF)],
        ),
        out_shape=jax.ShapeDtypeStruct((experts, cap, hidden), BF),
        cost_estimate=pl.CostEstimate(
            flops=4 * experts * main * width * hidden,
            bytes_accessed=4 * experts * width * hidden,
            transcendentals=experts * main * hidden,
        ),
        name="inner",
    )(scal, x_own, x_oth, rank, w_gate, w_gate, w_up, w_up)


def outer_kernel(scal, inner, rank, rank_t, gate, wd, out, hot, hot_t, slot_gate, total, *, main, cap):
    experts = wd.shape[0]
    tokens = rank.shape[1]

    def prepare(e, first, count):
        marks = hot_rows(rank[e : e + 1, :], first, count)
        slot_gate[e, first : first + count, :] = jnp.sum(
            jnp.where(marks, gate[e : e + 1, :], 0.0), axis=1, keepdims=True
        )
        lanes = lax.broadcasted_iota(jnp.int32, (tokens, count), 1) + first
        return (lanes == rank_t[:, e : e + 1]).astype(BF)

    def product(e, first, count):
        value = jnp.dot(inner[e, first : first + count, :], wd[e], preferred_element_type=F32)
        return (value * slot_gate[e, first : first + count, :]).astype(BF)

    @pl.when(pl.program_id(0) == 0)
    def _():
        for e in range(experts):
            hot[:, e * main : (e + 1) * main] = prepare(e, 0, main)

    sums = jnp.concatenate([product(e, 0, main) for e in range(experts)], axis=0)
    total[...] = jnp.dot(hot[...], sums, preferred_element_type=F32)
    if cap > main:
        for e in range(experts):

            @pl.when(scal[1 + e] > main)
            def _():
                hot_t[...] = prepare(e, main, cap - main)
                total[...] += jnp.dot(
                    hot_t[...], product(e, main, cap - main), preferred_element_type=F32
                )

    out[...] = total[...].astype(BF)


def expert_outer(scal, inner, rank, rank_t, gate, w_down, other, main, cap):
    experts, hidden, width = w_down.shape
    half, tokens = width // 2, rank.shape[1]
    block = min(256, half)
    blocks = half // block
    if other:
        where = lambda n, s: (0, 0, (1 - s[0]) * blocks + n)
    else:
        where = lambda n, s: (0, 0, s[0] * blocks + n)
    return pl.pallas_call(
        functools.partial(outer_kernel, main=main, cap=cap),
        grid_spec=pltpu.PrefetchScalarGridSpec(
            num_scalar_prefetch=1,
            grid=(blocks,),
            in_specs=[
                pl.BlockSpec((experts, cap, hidden), lambda n, s: (0, 0, 0)),
                pl.BlockSpec((experts, tokens), lambda n, s: (0, 0)),
                pl.BlockSpec((tokens, experts), lambda n, s: (0, 0)),
                pl.BlockSpec((experts, tokens), lambda n, s: (0, 0)),
                pl.BlockSpec((experts, hidden, block), where),
            ],
            out_specs=pl.BlockSpec((tokens, block), lambda n, s: (0, n)),
            scratch_shapes=[
                pltpu.VMEM((tokens, experts * main), BF),
                pltpu.VMEM((tokens, max(cap - main, 8)), BF),
                pltpu.VMEM((experts, cap, 1), F32),
                pltpu.VMEM((tokens, block), F32),
            ],
        ),
        out_shape=jax.ShapeDtypeStruct((tokens, half), BF),
        cost_estimate=pl.CostEstimate(
            flops=2 * experts * main * (hidden + tokens) * half,
            bytes_accessed=2 * experts * hidden * half,
            transcendentals=0,
        ),
        name="outer",
    )(scal, inner, rank, rank_t, gate, w_down)


def wide_experts(section, x_own, x_oth, rank, gate, w_gate, w_up, w_down, cap):
    half = x_oth.shape[1]
    first = section == 0
    rows = jnp.concatenate(
        [jnp.where(first, x_own, x_oth), jnp.where(first, x_oth, x_own)], axis=1
    )
    tokens, width = rows.shape
    total = jnp.zeros((tokens, width), F32)
    for e in range(w_gate.shape[0]):
        hot = hot_rows(rank[e : e + 1, :], 0, cap)
        slot_gate = jnp.sum(jnp.where(hot, gate[e : e + 1, :], 0.0), axis=1, keepdims=True)
        hot = hot.astype(BF)
        picked = jnp.dot(hot, rows, preferred_element_type=F32).astype(BF)
        g = jnp.dot(picked, w_gate[e], preferred_element_type=F32)
        u = jnp.dot(picked, w_up[e], preferred_element_type=F32)
        inner = (jax.nn.silu(g) * u).astype(BF)
        value = jnp.dot(inner, w_down[e], preferred_element_type=F32)
        value = (value * slot_gate).astype(BF)
        total = total + jnp.dot(hot.T, value, preferred_element_type=F32)
    total = total.astype(BF)
    own = lax.dynamic_slice_in_dim(total, section * half, half, 1)
    oth = lax.dynamic_slice_in_dim(total, (1 - section) * half, half, 1)
    return own, oth


def attention(query, keys, values, residual):
    token_count, half_width = query.shape
    kv_width = keys.shape[1]
    both = jnp.concatenate([keys, values], axis=1)
    steps = bits_of("tensor", 0)
    both = gather_all(both, steps)
    length = both.shape[0]
    me = lax.axis_index("tensor")
    order = jnp.zeros((1,), jnp.int32)
    for axis, mask in steps:
        order = jnp.concatenate([order, order ^ mask])
    source = me ^ order
    key_positions = (source[:, None] * token_count + jnp.arange(token_count)[None, :]).reshape(-1)
    local_kv = kv_width // HD
    groups = half_width // kv_width
    queries = query.reshape(token_count, local_kv, groups, HD)
    key_heads = both[:, :kv_width].reshape(length, local_kv, HD)
    value_heads = both[:, kv_width:].reshape(length, local_kv, HD)
    scores = jnp.einsum(
        "qkgd,tkd->kgqt", queries, key_heads, preferred_element_type=F32
    ) / math.sqrt(HD)
    query_positions = me * token_count + jnp.arange(token_count)
    causal = query_positions[:, None] >= key_positions[None, :]
    masked = jnp.where(causal, scores, -1e30)
    row_peak = jnp.max(masked, axis=-1, keepdims=True)
    exp_terms = jnp.where(causal, jnp.exp(masked - row_peak), 0.0)
    weights = (exp_terms / jnp.sum(exp_terms, axis=-1, keepdims=True)).astype(BF)
    context = jnp.einsum("kgqt,tkd->qkgd", weights, value_heads, preferred_element_type=F32)
    return (residual.astype(F32) + context.reshape(token_count, half_width)).astype(BF)


def on_device(query, keys, values, residual, routes, gates, w_gate, w_up, w_down):
    section = lax.axis_index("section")
    hidden = attention(query[0], keys[0], values[0], residual[0])
    token_count, half = hidden.shape
    share = token_count // 2
    experts = w_gate.shape[0]

    def rows_of(value, part):
        return lax.dynamic_slice_in_dim(value, part * share, share, 0)

    gate_high = lax.reduce_precision(gates[0], 8, 7)
    gate_mid = lax.reduce_precision(gates[0] - gate_high, 8, 7)
    gate_low = gates[0] - gate_high - gate_mid
    meta = jnp.concatenate([routes[0].astype(F32), gate_high, gate_mid, gate_low], axis=1)
    meta = jnp.pad(meta, ((0, 0), (0, META - meta.shape[1]))).astype(BF)

    steps = gather_steps()
    sent = rows_of(hidden, 1 - section)
    came = swap(sent, "section", 1)
    x_own = gather_all(rows_of(jnp.concatenate([hidden, meta], axis=1), section), steps)
    x_oth = gather_all(came, steps)

    tokens = x_oth.shape[0]
    info = x_own[:, half : half + 4 * TOP].astype(F32).T
    picked = info[:TOP]
    gate_all = info[TOP : 2 * TOP] + info[2 * TOP : 3 * TOP] + info[3 * TOP : 4 * TOP]
    ids = (lax.axis_index("expert") * experts + jnp.arange(experts)).astype(F32)
    hits = picked[None, :, :] == ids[:, None, None]
    match = jnp.any(hits, axis=1)
    gate = jnp.sum(jnp.where(hits, gate_all[None], 0.0), axis=1)
    lower = jnp.arange(tokens)[:, None] < jnp.arange(tokens)[None, :]
    before = jnp.dot(match.astype(BF), lower.astype(BF), preferred_element_type=F32)
    rank = jnp.where(match, before, -1.0).astype(jnp.int32)
    counts = jnp.sum(match, axis=1).astype(jnp.int32)
    scal = jnp.concatenate([section[None].astype(jnp.int32), counts])
    cap = tokens // share * min(CAP, share)
    main = min(cap, -(-tokens * TOP * 5 // (EXPERTS * 4)) // 16 * 16)

    if tokens <= 1024:
        inner = expert_inner(scal, x_own, x_oth, rank, w_gate, w_up, main, cap)
        pack = (scal, inner, rank, rank.T, gate, w_down)
        sum_oth = expert_outer(*pack, True, main, cap)
        sum_own = expert_outer(*pack, False, main, cap)
    else:
        sum_own, sum_oth = wide_experts(
            section, x_own[:, :half], x_oth, rank, gate, w_gate, w_up, w_down, cap
        )
    sum_oth = scatter_sum(sum_oth, steps)
    partner = swap(sum_oth, "section", 1)
    sum_own = scatter_sum(sum_own, steps)
    first = section == 0
    expert_sum = jnp.concatenate(
        [jnp.where(first, sum_own, partner), jnp.where(first, partner, sum_own)], axis=0
    )
    return (hidden.astype(F32) + expert_sum.astype(F32)).astype(BF)[None]


def solution(mesh):
    return jax.shard_map(
        on_device,
        mesh=mesh,
        in_specs=(
            P("expert", "tensor", "section"),
            P("expert", "tensor", "section"),
            P("expert", "tensor", "section"),
            P("expert", "tensor", "section"),
            P("expert", "tensor", None),
            P("expert", "tensor", None),
            P("expert", None, "tensor"),
            P("expert", None, "tensor"),
            P("expert", "tensor", None),
        ),
        out_specs=P("expert", "tensor", "section"),
        check_vma=False,
    )
```

time: 325 us -> 205 us (0.63)
  waiting for transfers between devices: 170 us -> 87.1 us
  Pallas kernels: 0 us -> 63.1 us
  blocking collectives: 56.7 us -> 0 us
  matrix products: 59.8 us -> 4.47 us
  starting transfers between devices: 5.4 us -> 29.8 us
  between operations: 14.2 us -> 0.41 us
  other arithmetic: 1.57 us -> 8.04 us
  local copies, waits for them, and re-layouts: 16.9 us -> 11.4 us
    unnamed x3 -> x0, waiting for transfers between devices: 103 us -> none
    ppermute x1 -> x21, waiting for transfers between devices: 6.06 us -> 87.1 us  [swap(): return lax.ppermute(value, axis, pairs)]
    pallas_call x0 -> x3, Pallas kernels: none -> 63.1 us  [the longest x1 34 us: expert_inner(): pl.pallas_call(functools.partial(inner_kernel, main=main, cap=cap), grid_...]
    dot_general x5 -> x2, matrix products: 57.5 us -> 2.26 us  [the longest x1 2.08 us: attention(): jnp.einsum('kgqt,tkd->qkgd', weights, value_heads, preferred_element_type...]
    all_gather x1 -> x0, waiting for transfers between devices: 51.6 us -> none  [on_device(): lax.all_gather(arrived, 'tensor', axis=0, tiled=True)]
    all_gather x3 -> x0, blocking collectives: 40.7 us -> none  [the longest x1 16.7 us: on_device(): lax.all_gather(keys, 'tensor', axis=1, tiled=True)]
    ppermute x1 -> x21, starting transfers between devices: 1.54 us -> 29.8 us  [swap(): return lax.ppermute(value, axis, pairs)]
    all_to_all x1 -> x0, blocking collectives: 16 us -> none  [on_device(): lax.all_to_all(packed, 'expert', split_axis=1, concat_axis=0, tiled=True)]
  transfers between devices with their start and end apart: 4 -> 21, of which waited for: 4 -> 14; matrix products, arithmetic and copies ran while one was open for 0% -> 5% of each run, Pallas kernels for 0% -> 7%
where the time goes in v1:
time: 205 us; the launch traced here: 204 us
  waiting for transfers between devices  87.1 us (42%)
  Pallas kernels  63.1 us (31%)
  starting transfers between devices  29.8 us (15%)
  local copies, waits for them, and re-layouts  11.4 us (6%)
  other arithmetic  8.04 us (4%)
  matrix products  4.47 us (2%)
    ppermute x21, waiting for transfers between devices, swap(): return lax.ppermute(value, axis, pairs)  87.1 us
    pallas_call x1, Pallas kernels, expert_inner(): pl.pallas_call(functools.partial(inner_kernel, main=main, cap=cap), grid_...  34 us
    ppermute x21, starting transfers between devices, swap(): return lax.ppermute(value, axis, pairs)  29.8 us
    pallas_call x2, Pallas kernels, expert_outer(): pl.pallas_call(functools.partial(outer_kernel, main=main, cap=cap), grid_...  29.2 us
  transfers between devices with their start and end apart: 21, of which 14 were waited for; matrix products, arithmetic and copies ran while one was open for 5% of the time, Pallas kernels for 7%

profile of v1, /device:TPU:0, one launch (start us, length us, event | category | flops | bytes accessed | tf_op | source)
XLA Modules:
  0.0 204.4 jit_solution(2897961641461492479)
XLA Ops:
  0.0 1.0 copy.67
  1.0 1.0 copy.68
  2.0 4.1 %collective-permute-start = (bf16[64,1024]{0,1:T(8,128)(2,1)S(1)}, bf16[64,1024]{0,1:T(8,128)(2,1)S(1)}, u32[]{:S(2)}, u32[]{:S(2)}) collective-permute-start(bf16[64,1024]{0,1:T(8,128)(2,1)S(1)} %pad_maximum_fusion.7), channel_id=1, source_target_pairs={{0,4},{1,5},{2,6},{3,7},{4,0},{5,1},{6,2},{7,3},{8,12},{9,13},{10,... | collective-permute-start | bytes 393224 | tf_op jit(solution)/shard_map/ppermute | solution.py:22
  6.2 0.7 xor_multiply_fusion
  6.9 11.2 %collective-permute-done = bf16[64,1024]{0,1:T(8,128)(2,1)S(1)} collective-permute-done((bf16[64,1024]{0,1:T(8,128)(2,1)S(1)}, bf16[64,1024]{0,1:T(8,128)(2,1)S(1)}, u32[]{:S(2)}, u32[]{:S(2)}) %collective-permute-start) | collective-permute-done | bytes 131104 | tf_op jit(solution)/shard_map/ppermute | solution.py:22
  18.1 0.1 pad_maximum_fusion.8
  18.2 0.8 collective-permute-start.1
  19.0 0.7 fusion.19
  19.8 0.7 reduce-precision_convert_fusion.1
  20.5 5.3 %collective-permute-done.1 = bf16[128,1024]{0,1:T(8,128)(2,1)S(1)} collective-permute-done((bf16[128,1024]{0,1:T(8,128)(2,1)S(1)}, bf16[128,1024]{0,1:T(8,128)(2,1)S(1)}, u32[]{:S(2)}, u32[]{:S(2)}) %collective-permute-start.1) | collective-permute-done | bytes 262176 | tf_op jit(solution)/shard_map/ppermute | solution.py:22
  25.8 0.2 pad_maximum_fusion.4
  26.2 0.2 reshape_squeeze.3
  26.5 1.5 collective-permute-done.2
  28.0 0.3 pad_maximum_fusion.1
  28.3 2.2 %fusion.26 = (f32[4,4,64]{2,1,0:T(4,128)S(1)}, f32[4,4,64,512]{3,2,1,0:T(8,128)}) fusion(pred[64,512]{1,0:T(8,128)(4,1)S(1)} %broadcast_compare_fusion, bf16[512,4,128,1]{0,2,3,1:T(8,128)(2,1)S(1)} %bitcast.58, bf16[64,4,4,128]{3,2,1,0:T(4,128)(2,1)S(1)} %reshape_squeeze.3), kind=kOutput, calls=%fused_computation.80 | convolution fusion | flops 136839680 | bytes 2920448 | tf_op jit(solution)/shard_map/sub | solution.py:244
  30.5 2.1 %convolution_bitcast_fusion = f32[64,4,4,128]{3,0,2,1:T(8,128)S(1)} fusion(bf16[512,4,128,1]{0,2,3,1:T(8,128)(2,1)S(1)} %bitcast.57, f32[4,4,64,512]{3,2,1,0:T(8,128)} %get-tuple-element.17, f32[4,4,64]{2,1,0:T(4,128)S(1)} %get-tuple-element.16), kind=kOutput, calls=%fused_computation.7 | convolution fusion | flops 135266304 | bytes 3149824 | tf_op jit(solution)/shard_map/kgqt,tkd->qkgd/dot_general | solution.py:246
  32.6 0.3 copy.72
  33.0 0.2 reshape.78
  33.2 0.4 copy-done.4
  33.7 1.4 collective-permute-start.7
  35.1 3.4 %collective-permute-start.3 = (bf16[32,2176]{1,0:T(8,128)(2,1)S(1)}, bf16[32,2176]{1,0:T(8,128)(2,1)S(1)}, u32[]{:S(2)}, u32[]{:S(2)}) collective-permute-start(bf16[32,2176]{1,0:T(8,128)(2,1)S(1)} %get-tuple-element.6), channel_id=1, source_target_pairs={{0,4},{1,5},{2,6},{3,7},{4,0},{5,1},{6,2},{7,3},{8,12},{9,13},{10,... | collective-permute-start | bytes 417800 | tf_op jit(solution)/shard_map/ppermute | solution.py:22
  38.5 0.8 collective-permute-done.7
  39.3 3.1 %collective-permute-start.8 = (bf16[32,2048]{1,0:T(8,128)(2,1)S(1)}, bf16[32,2048]{1,0:T(8,128)(2,1)S(1)}, u32[]{:S(2)}, u32[]{:S(2)}) collective-permute-start(bf16[32,2048]{1,0:T(8,128)(2,1)S(1)} %collective-permute-done.7), channel_id=1, source_target_pairs={{0,4},{1,5},{2,6},{3,7},{4,0},{5,1},{6,2},{7,3},{8,12},{9,13},{10,... | collective-permute-start | bytes 393224 | tf_op jit(solution)/shard_map/ppermute | solution.py:22
  42.4 6.4 %collective-permute-done.3 = bf16[32,2176]{1,0:T(8,128)(2,1)S(1)} collective-permute-done((bf16[32,2176]{1,0:T(8,128)(2,1)S(1)}, bf16[32,2176]{1,0:T(8,128)(2,1)S(1)}, u32[]{:S(2)}, u32[]{:S(2)}) %collective-permute-start.3) | collective-permute-done | bytes 139296 | tf_op jit(solution)/shard_map/ppermute | solution.py:22
  48.9 1.9 collective-permute-done.8
  50.9 0.7 collective-permute-start.9
  51.6 6.8 %collective-permute-done.4 = bf16[64,2176]{1,0:T(8,128)(2,1)S(1)} collective-permute-done((bf16[64,2176]{1,0:T(8,128)(2,1)S(1)}, bf16[64,2176]{1,0:T(8,128)(2,1)S(1)}, u32[]{:S(2)}, u32[]{:S(2)}) %collective-permute-start.4) | collective-permute-done | bytes 278560 | tf_op jit(solution)/shard_map/ppermute | solution.py:22
  58.4 1.6 collective-permute-start.5
  60.0 9.8 %collective-permute-done.5 = bf16[128,2176]{1,0:T(8,128)(2,1)S(1)} collective-permute-done((bf16[128,2176]{1,0:T(8,128)(2,1)S(1)}, bf16[128,2176]{1,0:T(8,128)(2,1)S(1)}, u32[]{:S(2)}, u32[]{:S(2)}) %collective-permute-start.5) | collective-permute-done | bytes 557088 | tf_op jit(solution)/shard_map/ppermute | solution.py:22
  70.0 1.5 collective-permute-start.10
  71.7 12.8 %collective-permute-done.10 = bf16[128,2048]{1,0:T(8,128)(2,1)S(1)} collective-permute-done((bf16[128,2048]{1,0:T(8,128)(2,1)S(1)}, bf16[128,2048]{1,0:T(8,128)(2,1)S(1)}, u32[]{:S(2)}, u32[]{:S(2)}) %collective-permute-start.10) | collective-permute-done | bytes 524320 | tf_op jit(solution)/shard_map/ppermute | solution.py:22
  84.4 1.0 pad_maximum_fusion.2
  85.5 0.1 constant_dynamic-update-slice_fusion.x_own
  85.7 0.3 slice_add_fusion
  86.0 0.9 copy-done.3
  87.2 0.2 fusion.2.rank
  87.4 0.9 copy.76
  88.4 0.6 pad_add_fusion.scal
  89.0 0.7 fusion.17.gate
  89.7 2.3 %constant_dynamic-update-slice_fusion.5.x_oth = bf16[512,2048]{1,0:T(8,128)(2,1)} fusion(bf16[512,2048]{1,0:T(8,128)(2,1)} %copy-done.3, bf16[256,2048]{1,0:T(8,128)(2,1)} %collective-permute-done.11), kind=kLoop, calls=%fused_computation.54 | loop fusion | bytes 2097152 | tf_op jit(solution)/shard_map/concatenate | solution.py:36
  92.0 34.0 %inner.1 = bf16[4,272,1024]{2,1,0:T(8,128)(2,1)} custom-call(s32[5]{0:T(128)} %pad_add_fusion.scal, bf16[512,2176]{1,0:T(8,128)(2,1)} %copy-done.2, bf16[512,2048]{1,0:T(8,128)(2,1)} %constant_dynamic-update-slice_fusion.5.x_oth, s32[4,512]{1,0:T(4,128)} %copy-done.6, bf16[4,4096,1024]{2,1,0:T(8,128)(2,1)} %wg_oth.1, bf16[4,4096,1024]{2,1,0:T(8,128)(2,1)} %wg_oth.1, ...), custom_call_target="tpu_custom_call" | custom-call | flops 10737418240 | bytes 67108864 | tf_op jit(solution)/shard_map/inner/pallas_call | solution.py:92
  126.0 14.6 %outer.3 = bf16[512,2048]{1,0:T(8,128)(2,1)} custom-call(s32[5]{0:T(128)} %pad_add_fusion.scal, bf16[4,272,1024]{2,1,0:T(8,128)(2,1)} %inner.1, s32[4,512]{1,0:T(4,128)} %copy-done.6, s32[512,4]{1,0:T(8,128)} %bitcast.55, f32[4,512]{1,0:T(4,128)} %fusion.17.gate, bf16[4,1024,4096]{2,1,0:T(8,128)(2,1)} %wd.3), custom_call_target="tpu_custom_call" | custom-call | flops 4026531840 | bytes 16777216 | tf_op jit(solution)/shard_map/outer/pallas_call | solution.py:164
  140.6 1.3 slice.108
  141.9 0.6 collective-permute-start.16
  142.5 14.5 %outer.2 = bf16[512,2048]{1,0:T(8,128)(2,1)} custom-call(s32[5]{0:T(128)} %pad_add_fusion.scal, bf16[4,272,1024]{2,1,0:T(8,128)(2,1)} %inner.1, s32[4,512]{1,0:T(4,128)} %copy-done.6, s32[512,4]{1,0:T(8,128)} %bitcast.56, f32[4,512]{1,0:T(4,128)} %fusion.17.gate, bf16[4,1024,4096]{2,1,0:T(8,128)(2,1)} %wd.3), custom_call_target="tpu_custom_call" | custom-call | flops 4026531840 | bytes 16777216 | tf_op jit(solution)/shard_map/outer/pallas_call | solution.py:164
  157.0 1.4 slice.100
  158.6 0.4 copy-done.1
  158.9 0.4 add_convert_fusion
  159.4 1.5 collective-permute-start.17
  160.9 0.3 collective-permute-done.12
  161.2 0.4 add_convert_fusion.1
  161.6 1.5 collective-permute-start.13
  163.2 11.0 %collective-permute-done.17 = bf16[128,2048]{1,0:T(8,128)(2,1)S(1)} collective-permute-done((bf16[128,2048]{1,0:T(8,128)(2,1)S(1)}, bf16[128,2048]{1,0:T(8,128)(2,1)S(1)}, u32[]{:S(2)}, u32[]{:S(2)}) %collective-permute-start.17) | collective-permute-done | bytes 524320 | tf_op jit(solution)/shard_map/ppermute | solution.py:22
  174.2 0.1 add_convert_fusion.2
  174.4 1.3 collective-permute-start.18
  175.7 9.0 %collective-permute-done.13 = bf16[128,2048]{1,0:T(8,128)(2,1)S(1)} collective-permute-done((bf16[128,2048]{1,0:T(8,128)(2,1)S(1)}, bf16[128,2048]{1,0:T(8,128)(2,1)S(1)}, u32[]{:S(2)}, u32[]{:S(2)}) %collective-permute-start.13) | collective-permute-done | bytes 524320 | tf_op jit(solution)/shard_map/ppermute | solution.py:22
  184.8 1.3 collective-permute-start.14
  186.2 3.7 %collective-permute-start.19 = (bf16[32,2048]{1,0:T(8,128)(2,1)S(1)}, bf16[32,2048]{1,0:T(8,128)(2,1)S(1)}, u32[]{:S(2)}, u32[]{:S(2)}) collective-permute-start(bf16[32,2048]{1,0:T(8,128)(2,1)S(1)} %slice.114), channel_id=1, source_target_pairs={{0,4},{1,5},{2,6},{3,7},{4,0},{5,1},{6,2},{7,3},{8,12},{9,13},{10,... | collective-permute-start | bytes 393224 | tf_op jit(solution)/shard_map/ppermute | solution.py:22
  189.8 5.3 %collective-permute-done.14 = bf16[64,2048]{1,0:T(8,128)(2,1)S(1)} collective-permute-done((bf16[64,2048]{1,0:T(8,128)(2,1)S(1)}, bf16[64,2048]{1,0:T(8,128)(2,1)S(1)}, u32[]{:S(2)}, u32[]{:S(2)}) %collective-permute-start.14) | collective-permute-done | bytes 262176 | tf_op jit(solution)/shard_map/ppermute | solution.py:22
  195.2 2.4 %collective-permute-start.15 = (bf16[32,2048]{1,0:T(8,128)(2,1)S(1)}, bf16[32,2048]{1,0:T(8,128)(2,1)S(1)}, u32[]{:S(2)}, u32[]{:S(2)}) collective-permute-start(bf16[32,2048]{1,0:T(8,128)(2,1)S(1)} %slice.106), channel_id=1, source_target_pairs={{0,4},{1,5},{2,6},{3,7},{4,0},{5,1},{6,2},{7,3},{8,12},{9,13},{10,... | collective-permute-start | bytes 393224 | tf_op jit(solution)/shard_map/ppermute | solution.py:22
  197.7 0.6 collective-permute-start.20
  198.2 0.2 reshape.77
  198.5 5.1 %collective-permute-done.15 = bf16[32,2048]{1,0:T(8,128)(2,1)S(1)} collective-permute-done((bf16[32,2048]{1,0:T(8,128)(2,1)S(1)}, bf16[32,2048]{1,0:T(8,128)(2,1)S(1)}, u32[]{:S(2)}, u32[]{:S(2)}) %collective-permute-start.15) | collective-permute-done | bytes 131104 | tf_op jit(solution)/shard_map/ppermute | solution.py:22
  203.6 0.8 add_convert_fusion.4
  (63 shorter events, 2.2 us)
Async XLA Ops:
  0.0 26.2 %copy-start.5 = (bf16[1,64,2048]{2,1,0:T(8,128)(2,1)S(1)}, bf16[1,64,2048]{2,1,0:T(8,128)(2,1)}, u32[]{:S(2)}) copy-start(bf16[1,64,2048]{2,1,0:T(8,128)(2,1)} %param.9) | copy-start | bytes 786436
  2.0 16.1 %collective-permute-start = (bf16[64,1024]{0,1:T(8,128)(2,1)S(1)}, bf16[64,1024]{0,1:T(8,128)(2,1)S(1)}, u32[]{:S(2)}, u32[]{:S(2)}) collective-permute-start(bf16[64,1024]{0,1:T(8,128)(2,1)S(1)} %pad_maximum_fusion.7), channel_id=1, source_target_pairs={{0,4},{1,5},{2,6},{3,7},{4,0},{5,1},{6,2},{7,3},{8,12},{9,13},{10,... | collective-permute-start | bytes 393224 | tf_op jit(solution)/shard_map/ppermute | solution.py:22
  18.2 7.5 %collective-permute-start.1 = (bf16[128,1024]{0,1:T(8,128)(2,1)S(1)}, bf16[128,1024]{0,1:T(8,128)(2,1)S(1)}, u32[]{:S(2)}, u32[]{:S(2)}) collective-permute-start(bf16[128,1024]{0,1:T(8,128)(2,1)S(1)} %pad_maximum_fusion.8), channel_id=1, source_target_pairs={{0,2},{1,3},{2,0},{3,1},{4,6},{5,7},{6,4},{7,5},{8,10},{9,11},{10,... | collective-permute-start | bytes 786440 | tf_op jit(solution)/shard_map/ppermute | solution.py:22
  26.0 2.0 collective-permute-start.2
  32.6 1.0 copy-start.4
  33.7 5.6 %collective-permute-start.7 = (bf16[32,2048]{1,0:T(8,128)(2,1)S(1)}, bf16[32,2048]{1,0:T(8,128)(2,1)S(1)}, u32[]{:S(2)}, u32[]{:S(2)}) collective-permute-start(bf16[32,2048]{1,0:T(8,128)(2,1)S(1)} %constant_dynamic-slice_fusion), channel_id=1, source_target_pairs={{0,16},{16,0},{1,17},{17,1},{2,18},{18,2},{3,19},{19,3},{4,20},{20... | collective-permute-start | bytes 393224 | tf_op jit(solution)/shard_map/ppermute | solution.py:22
  35.1 13.7 %collective-permute-start.3 = (bf16[32,2176]{1,0:T(8,128)(2,1)S(1)}, bf16[32,2176]{1,0:T(8,128)(2,1)S(1)}, u32[]{:S(2)}, u32[]{:S(2)}) collective-permute-start(bf16[32,2176]{1,0:T(8,128)(2,1)S(1)} %get-tuple-element.6), channel_id=1, source_target_pairs={{0,4},{1,5},{2,6},{3,7},{4,0},{5,1},{6,2},{7,3},{8,12},{9,13},{10,... | collective-permute-start | bytes 417800 | tf_op jit(solution)/shard_map/ppermute | solution.py:22
  39.3 11.6 %collective-permute-start.8 = (bf16[32,2048]{1,0:T(8,128)(2,1)S(1)}, bf16[32,2048]{1,0:T(8,128)(2,1)S(1)}, u32[]{:S(2)}, u32[]{:S(2)}) collective-permute-start(bf16[32,2048]{1,0:T(8,128)(2,1)S(1)} %collective-permute-done.7), channel_id=1, source_target_pairs={{0,4},{1,5},{2,6},{3,7},{4,0},{5,1},{6,2},{7,3},{8,12},{9,13},{10,... | collective-permute-start | bytes 393224 | tf_op jit(solution)/shard_map/ppermute | solution.py:22
  48.8 9.6 %collective-permute-start.4 = (bf16[64,2176]{1,0:T(8,128)(2,1)S(1)}, bf16[64,2176]{1,0:T(8,128)(2,1)S(1)}, u32[]{:S(2)}, u32[]{:S(2)}) collective-permute-start(bf16[64,2176]{1,0:T(8,128)(2,1)S(1)} %pad_maximum_fusion.6), channel_id=1, source_target_pairs={{0,2},{1,3},{2,0},{3,1},{4,6},{5,7},{6,4},{7,5},{8,10},{9,11},{10,... | collective-permute-start | bytes 835592 | tf_op jit(solution)/shard_map/ppermute | solution.py:22
  50.9 19.1 %collective-permute-start.9 = (bf16[64,2048]{1,0:T(8,128)(2,1)S(1)}, bf16[64,2048]{1,0:T(8,128)(2,1)S(1)}, u32[]{:S(2)}, u32[]{:S(2)}) collective-permute-start(bf16[64,2048]{1,0:T(8,128)(2,1)S(1)} %pad_maximum_fusion.9), channel_id=1, source_target_pairs={{0,2},{1,3},{2,0},{3,1},{4,6},{5,7},{6,4},{7,5},{8,10},{9,11},{10,... | collective-permute-start | bytes 786440 | tf_op jit(solution)/shard_map/ppermute | solution.py:22
  58.4 11.4 %collective-permute-start.5 = (bf16[128,2176]{1,0:T(8,128)(2,1)S(1)}, bf16[128,2176]{1,0:T(8,128)(2,1)S(1)}, u32[]{:S(2)}, u32[]{:S(2)}) collective-permute-start(bf16[128,2176]{1,0:T(8,128)(2,1)S(1)} %pad_maximum_fusion.3), channel_id=1, source_target_pairs={{0,8},{8,0},{1,9},{9,1},{2,10},{10,2},{3,11},{11,3},{4,12},{12,4},... | collective-permute-start | bytes 1671176 | tf_op jit(solution)/shard_map/ppermute | solution.py:22
  69.9 15.6 %collective-permute-start.6 = (bf16[256,2176]{1,0:T(8,128)(2,1)S(1)}, bf16[256,2176]{1,0:T(8,128)(2,1)S(1)}, u32[]{:S(2)}, u32[]{:S(2)}) collective-permute-start(bf16[256,2176]{1,0:T(8,128)(2,1)S(1)} %pad_maximum_fusion), channel_id=1, source_target_pairs={{0,1},{1,0},{2,3},{3,2},{4,5},{5,4},{6,7},{7,6},{8,9},{9,8},{10,11... | collective-permute-start | bytes 3342344 | tf_op jit(solution)/shard_map/ppermute | solution.py:22
  70.0 14.4 %collective-permute-start.10 = (bf16[128,2048]{1,0:T(8,128)(2,1)S(1)}, bf16[128,2048]{1,0:T(8,128)(2,1)S(1)}, u32[]{:S(2)}, u32[]{:S(2)}) collective-permute-start(bf16[128,2048]{1,0:T(8,128)(2,1)S(1)} %pad_maximum_fusion.5), channel_id=1, source_target_pairs={{0,8},{8,0},{1,9},{9,1},{2,10},{10,2},{3,11},{11,3},{4,12},{12,4},... | collective-permute-start | bytes 1572872 | tf_op jit(solution)/shard_map/ppermute | solution.py:22
  85.5 4.2 %collective-permute-start.11 = (bf16[256,2048]{1,0:T(8,128)(2,1)}, bf16[256,2048]{1,0:T(8,128)(2,1)}, u32[]{:S(2)}, u32[]{:S(2)}) collective-permute-start(bf16[256,2048]{1,0:T(8,128)(2,1)} %pad_maximum_fusion.2), channel_id=1, source_target_pairs={{0,1},{1,0},{2,3},{3,2},{4,5},{5,4},{6,7},{7,6},{8,9},{9,8},{10,11... | collective-permute-start | bytes 3145736 | tf_op jit(solution)/shard_map/ppermute | solution.py:22
  85.5 1.4 copy-start.3
  85.7 6.3 %copy-start.2 = (bf16[512,2176]{1,0:T(8,128)(2,1)}, bf16[512,2176]{1,0:T(8,128)(2,1)S(1)}, u32[]{:S(2)}) copy-start(bf16[512,2176]{1,0:T(8,128)(2,1)S(1)} %constant_dynamic-update-slice_fusion.x_own) | copy-start | bytes 6684676
  87.4 4.6 %copy-start.6 = (s32[4,512]{1,0:T(4,128)}, s32[4,512]{1,0:T(4,128)S(1)}, u32[]{:S(2)}) copy-start(s32[4,512]{1,0:T(4,128)S(1)} %fusion.2.rank) | copy-start | bytes 24580
  141.9 16.7 %collective-permute-start.16 = (bf16[256,2048]{1,0:T(8,128)(2,1)S(1)}, bf16[256,2048]{1,0:T(8,128)(2,1)S(1)}, u32[]{:S(2)}, u32[]{:S(2)}) collective-permute-start(bf16[256,2048]{1,0:T(8,128)(2,1)S(1)} %slice.108), channel_id=1, source_target_pairs={{0,1},{1,0},{2,3},{3,2},{4,5},{5,4},{6,7},{7,6},{8,9},{9,8},{10,11... | collective-permute-start | bytes 3145736 | tf_op jit(solution)/shard_map/ppermute | solution.py:22
  157.0 1.9 copy-start.1
  158.5 2.7 %copy-start = (bf16[512,2048]{1,0:T(8,128)(2,1)S(1)}, bf16[512,2048]{1,0:T(8,128)(2,1)}, u32[]{:S(2)}) copy-start(bf16[512,2048]{1,0:T(8,128)(2,1)} %outer.2) | copy-start | bytes 6291460
  158.5 2.7 %collective-permute-start.12 = (bf16[256,2048]{1,0:T(8,128)(2,1)S(1)}, bf16[256,2048]{1,0:T(8,128)(2,1)S(1)}, u32[]{:S(2)}, u32[]{:S(2)}) collective-permute-start(bf16[256,2048]{1,0:T(8,128)(2,1)S(1)} %slice.100), channel_id=1, source_target_pairs={{0,1},{1,0},{2,3},{3,2},{4,5},{5,4},{6,7},{7,6},{8,9},{9,8},{10,11... | collective-permute-start | bytes 3145736 | tf_op jit(solution)/shard_map/ppermute | solution.py:22
  159.4 14.9 %collective-permute-start.17 = (bf16[128,2048]{1,0:T(8,128)(2,1)S(1)}, bf16[128,2048]{1,0:T(8,128)(2,1)S(1)}, u32[]{:S(2)}, u32[]{:S(2)}) collective-permute-start(bf16[128,2048]{1,0:T(8,128)(2,1)S(1)} %slice.110), channel_id=1, source_target_pairs={{0,8},{8,0},{1,9},{9,1},{2,10},{10,2},{3,11},{11,3},{4,12},{12,4},... | collective-permute-start | bytes 1572872 | tf_op jit(solution)/shard_map/ppermute | solution.py:22
  161.6 23.0 %collective-permute-start.13 = (bf16[128,2048]{1,0:T(8,128)(2,1)S(1)}, bf16[128,2048]{1,0:T(8,128)(2,1)S(1)}, u32[]{:S(2)}, u32[]{:S(2)}) collective-permute-start(bf16[128,2048]{1,0:T(8,128)(2,1)S(1)} %slice.102), channel_id=1, source_target_pairs={{0,8},{8,0},{1,9},{9,1},{2,10},{10,2},{3,11},{11,3},{4,12},{12,4},... | collective-permute-start | bytes 1572872 | tf_op jit(solution)/shard_map/ppermute | solution.py:22
  174.4 11.7 %collective-permute-start.18 = (bf16[64,2048]{1,0:T(8,128)(2,1)S(1)}, bf16[64,2048]{1,0:T(8,128)(2,1)S(1)}, u32[]{:S(2)}, u32[]{:S(2)}) collective-permute-start(bf16[64,2048]{1,0:T(8,128)(2,1)S(1)} %slice.112), channel_id=1, source_target_pairs={{0,2},{1,3},{2,0},{3,1},{4,6},{5,7},{6,4},{7,5},{8,10},{9,11},{10,... | collective-permute-start | bytes 786440 | tf_op jit(solution)/shard_map/ppermute | solution.py:22
  184.8 10.4 %collective-permute-start.14 = (bf16[64,2048]{1,0:T(8,128)(2,1)S(1)}, bf16[64,2048]{1,0:T(8,128)(2,1)S(1)}, u32[]{:S(2)}, u32[]{:S(2)}) collective-permute-start(bf16[64,2048]{1,0:T(8,128)(2,1)S(1)} %slice.104), channel_id=1, source_target_pairs={{0,2},{1,3},{2,0},{3,1},{4,6},{5,7},{6,4},{7,5},{8,10},{9,11},{10,... | collective-permute-start | bytes 786440 | tf_op jit(solution)/shard_map/ppermute | solution.py:22
  186.2 11.5 %collective-permute-start.19 = (bf16[32,2048]{1,0:T(8,128)(2,1)S(1)}, bf16[32,2048]{1,0:T(8,128)(2,1)S(1)}, u32[]{:S(2)}, u32[]{:S(2)}) collective-permute-start(bf16[32,2048]{1,0:T(8,128)(2,1)S(1)} %slice.114), channel_id=1, source_target_pairs={{0,4},{1,5},{2,6},{3,7},{4,0},{5,1},{6,2},{7,3},{8,12},{9,13},{10,... | collective-permute-start | bytes 393224 | tf_op jit(solution)/shard_map/ppermute | solution.py:22
  195.2 8.3 %collective-permute-start.15 = (bf16[32,2048]{1,0:T(8,128)(2,1)S(1)}, bf16[32,2048]{1,0:T(8,128)(2,1)S(1)}, u32[]{:S(2)}, u32[]{:S(2)}) collective-permute-start(bf16[32,2048]{1,0:T(8,128)(2,1)S(1)} %slice.106), channel_id=1, source_target_pairs={{0,4},{1,5},{2,6},{3,7},{4,0},{5,1},{6,2},{7,3},{8,12},{9,13},{10,... | collective-permute-start | bytes 393224 | tf_op jit(solution)/shard_map/ppermute | solution.py:22
  197.7 5.8 %collective-permute-start.20 = (bf16[32,2048]{1,0:T(8,128)(2,1)S(1)}, bf16[32,2048]{1,0:T(8,128)(2,1)S(1)}, u32[]{:S(2)}, u32[]{:S(2)}) collective-permute-start(bf16[32,2048]{1,0:T(8,128)(2,1)S(1)} %add_convert_fusion.7), channel_id=1, source_target_pairs={{0,16},{16,0},{1,17},{17,1},{2,18},{18,2},{3,19},{19,3},{4,20},{20... | collective-permute-start | bytes 393224 | tf_op jit(solution)/shard_map/ppermute | solution.py:22

commit v2 on v1

v2 whole, which is shorter than its diff:
```python
import functools
import math

import jax
import jax.numpy as jnp
from jax import lax
from jax.experimental import pallas as pl
from jax.experimental.pallas import tpu as pltpu
from jax.sharding import PartitionSpec as P


HD = 128
EXPERTS = 8
TOP = 2
CAP = 17
BF = jnp.bfloat16
F32 = jnp.float32


def swap(value, axis, mask):
    pairs = [(i, i ^ mask) for i in range(lax.axis_size(axis))]
    return lax.ppermute(value, axis, pairs)


def bits_of(axis, lowest):
    count = lax.axis_size(axis).bit_length() - 1
    return [(axis, 1 << b) for b in reversed(range(lowest, count))]


def gather_steps():
    return bits_of("tensor", 1) + bits_of("expert", 0) + [("tensor", 1)]


def named_swap(value, step):
    return swap(value, *step)


def gather_pair(block, steps):
    for step in steps[:-1]:
        block = jnp.concatenate([block, named_swap(block, step)], axis=0)
    return block, named_swap(block, steps[-1])


def gather_four(block, steps, also=()):
    for step in steps[:-2]:
        block = jnp.concatenate([block, named_swap(block, step)], axis=0)
    came = named_swap(block, steps[-2])
    beside = named_swap(block, steps[-1])
    if also:
        beside, also = lax.optimization_barrier((beside, also))
    return (block, came, beside, named_swap(came, steps[-1])), also


def add_rows(a, b):
    return (a.astype(F32) + b.astype(F32)).astype(BF)


def scatter_sum(near, far, steps):
    total = add_rows(near, named_swap(far, steps[-1]))
    for i in reversed(range(len(steps) - 1)):
        half = total.shape[0] // 2
        total = add_rows(total[:half], named_swap(total[half:], steps[i]))
    return total


def hot_rows(rank_row, first, count):
    slots = lax.broadcasted_iota(jnp.int32, (count, rank_row.shape[1]), 0) + first
    return slots == rank_row


def inner_kernel(scal, *refs, main, cap, split, final):
    pieces = refs[:4]
    rank, wg, wu = refs[4:7]
    rest = refs[7:]
    if final:
        (gate_in, up_in, gate_more, up_more), rest = rest[:4], rest[4:]
        out, rows, table = rest
    else:
        gate_out, up_out, gate_spill, up_spill, rows, table = rest
    e, n = pl.program_id(0), pl.program_id(1)

    @pl.when(jnp.logical_and(e == 0, n == 0))
    def _():
        for i, piece in enumerate(pieces):
            table[i * split : (i + 1) * split, :] = piece[...]

    def part(first, count):
        @pl.when(n == 0)
        def _():
            hot = hot_rows(rank[pl.ds(e, 1), :], first, count).astype(BF)
            rows[first : first + count, :] = jnp.dot(
                hot, table[...], preferred_element_type=F32
            ).astype(BF)

        picked = rows[first : first + count, :]
        gate = jnp.dot(picked, wg[0], preferred_element_type=F32)
        up = jnp.dot(picked, wu[0], preferred_element_type=F32)
        if final:
            gate = gate + (gate_more if first else gate_in)[0]
            up = up + (up_more if first else up_in)[0]
            out[0, first : first + count, :] = (gate / (1.0 + jnp.exp(-gate)) * up).astype(BF)
        else:
            (gate_spill if first else gate_out)[0] = gate
            (up_spill if first else up_out)[0] = up

    part(0, main)
    if cap > main:

        @pl.when(scal[1 + e] > main)
        def _():
            part(main, cap - main)


def expert_inner(scal, pieces, rank, w_gate, w_up, partial, main, cap):
    experts, width, hidden = w_gate.shape
    half, split = width // 2, pieces[0].shape[0]
    final = partial is not None
    block = min(1024, hidden)
    more = max(cap - main, 8)

    def spilled(e, s):
        return s[1 + e] > main

    rows_spec = pl.BlockSpec((split, half), lambda e, n, s: (0, 0))
    if final:
        w_spec = pl.BlockSpec((1, half, block), lambda e, n, s: (e, 1 - s[0], n))
    else:
        w_spec = pl.BlockSpec((1, half, block), lambda e, n, s: (e, s[0], n))
    main_spec = pl.BlockSpec((1, main, block), lambda e, n, s: (e, 0, n))
    more_spec = pl.BlockSpec(
        (1, more, block),
        lambda e, n, s: (
            jnp.where(spilled(e, s), e, experts),
            0,
            jnp.where(spilled(e, s), n, 0),
        ),
    )
    partial_specs = [main_spec, main_spec, more_spec, more_spec]
    partial_shapes = [jax.ShapeDtypeStruct((experts, main, hidden), F32)] * 2 + [
        jax.ShapeDtypeStruct((experts + 1, more, hidden), F32)
    ] * 2
    return pl.pallas_call(
        functools.partial(inner_kernel, main=main, cap=cap, split=split, final=final),
        grid_spec=pltpu.PrefetchScalarGridSpec(
            num_scalar_prefetch=1,
            grid=(experts, hidden // block),
            in_specs=[
                rows_spec,
                rows_spec,
                rows_spec,
                rows_spec,
                pl.BlockSpec(rank.shape, lambda e, n, s: (0, 0)),
                w_spec,
                w_spec,
            ]
            + (partial_specs if final else []),
            out_specs=(
                pl.BlockSpec((1, cap, block), lambda e, n, s: (e, 0, n)) if final else partial_specs
            ),
            scratch_shapes=[pltpu.VMEM((cap, half), BF), pltpu.VMEM((4 * split, half), BF)],
        ),
        out_shape=(
            jax.ShapeDtypeStruct((experts, cap, hidden), BF) if final else partial_shapes
        ),
        cost_estimate=pl.CostEstimate(
            flops=4 * experts * main * half * hidden,
            bytes_accessed=4 * experts * half * hidden,
            transcendentals=experts * main * hidden,
        ),
        compiler_params=pltpu.CompilerParams(vmem_limit_bytes=38 << 20),
        name="inner_last" if final else "inner_first",
    )(scal, *pieces, rank, w_gate, w_up, *(partial if final else ()))


def outer_kernel(
    scal, inner, rank, rank_t, gate, wd, near, far, hot, hot_t, slot_gate, total, *, main, cap
):
    experts = wd.shape[0]
    tokens = rank.shape[1]

    def prepare(e, first, count):
        marks = hot_rows(rank[e : e + 1, :], first, count)
        slot_gate[e, first : first + count, :] = jnp.sum(
            jnp.where(marks, gate[e : e + 1, :], 0.0), axis=1, keepdims=True
        )
        lanes = lax.broadcasted_iota(jnp.int32, (tokens, count), 1) + first
        return (lanes == rank_t[:, e : e + 1]).astype(BF)

    def product(e, first, count):
        value = jnp.dot(inner[e, first : first + count, :], wd[e], preferred_element_type=F32)
        return (value * slot_gate[e, first : first + count, :]).astype(BF)

    @pl.when(pl.program_id(0) == 0)
    def _():
        for e in range(experts):
            hot[:, e * main : (e + 1) * main] = prepare(e, 0, main)

    sums = jnp.concatenate([product(e, 0, main) for e in range(experts)], axis=0)
    total[...] = jnp.dot(hot[...], sums, preferred_element_type=F32)
    if cap > main:
        for e in range(experts):

            @pl.when(scal[1 + e] > main)
            def _():
                hot_t[...] = prepare(e, main, cap - main)
                total[...] += jnp.dot(
                    hot_t[...], product(e, main, cap - main), preferred_element_type=F32
                )

    near[...] = total[: tokens // 2, :].astype(BF)
    far[...] = total[tokens // 2 :, :].astype(BF)


def expert_outer(scal, inner, rank, rank_t, gate, w_down, other, main, cap):
    experts, hidden, width = w_down.shape
    half, tokens = width // 2, rank.shape[1]
    block = min(1024, half)
    blocks = half // block
    if other:
        where = lambda n, s: (0, 0, (1 - s[0]) * blocks + n)
    else:
        where = lambda n, s: (0, 0, s[0] * blocks + n)
    out_spec = pl.BlockSpec((tokens // 2, block), lambda n, s: (0, n))
    return pl.pallas_call(
        functools.partial(outer_kernel, main=main, cap=cap),
        grid_spec=pltpu.PrefetchScalarGridSpec(
            num_scalar_prefetch=1,
            grid=(blocks,),
            in_specs=[
                pl.BlockSpec((experts, cap, hidden), lambda n, s: (0, 0, 0)),
                pl.BlockSpec((experts, tokens), lambda n, s: (0, 0)),
                pl.BlockSpec((tokens, experts), lambda n, s: (0, 0)),
                pl.BlockSpec((experts, tokens), lambda n, s: (0, 0)),
                pl.BlockSpec((experts, hidden, block), where),
            ],
            out_specs=[out_spec, out_spec],
            scratch_shapes=[
                pltpu.VMEM((tokens, experts * main), BF),
                pltpu.VMEM((tokens, max(cap - main, 8)), BF),
                pltpu.VMEM((experts, cap, 1), F32),
                pltpu.VMEM((tokens, block), F32),
            ],
        ),
        out_shape=[jax.ShapeDtypeStruct((tokens // 2, half), BF)] * 2,
        cost_estimate=pl.CostEstimate(
            flops=2 * experts * main * (hidden + tokens) * half,
            bytes_accessed=2 * experts * hidden * half,
            transcendentals=0,
        ),
        compiler_params=pltpu.CompilerParams(vmem_limit_bytes=24 << 20),
        name="outer_other" if other else "outer_own",
    )(scal, inner, rank, rank_t, gate, w_down)


def wide_experts(section, x_own, x_oth, rank, gate, w_gate, w_up, w_down, cap):
    half = x_oth.shape[1]
    first = section == 0
    rows = jnp.concatenate(
        [jnp.where(first, x_own, x_oth), jnp.where(first, x_oth, x_own)], axis=1
    )
    tokens, width = rows.shape
    total = jnp.zeros((tokens, width), F32)
    for e in range(w_gate.shape[0]):
        hot = hot_rows(rank[e : e + 1, :], 0, cap)
        slot_gate = jnp.sum(jnp.where(hot, gate[e : e + 1, :], 0.0), axis=1, keepdims=True)
        hot = hot.astype(BF)
        picked = jnp.dot(hot, rows, preferred_element_type=F32).astype(BF)
        g = jnp.dot(picked, w_gate[e], preferred_element_type=F32)
        u = jnp.dot(picked, w_up[e], preferred_element_type=F32)
        inner = (jax.nn.silu(g) * u).astype(BF)
        value = jnp.dot(inner, w_down[e], preferred_element_type=F32)
        value = (value * slot_gate).astype(BF)
        total = total + jnp.dot(hot.T, value, preferred_element_type=F32)
    total = total.astype(BF)
    own = lax.dynamic_slice_in_dim(total, section * half, half, 1)
    oth = lax.dynamic_slice_in_dim(total, (1 - section) * half, half, 1)
    middle = tokens // 2
    return (own[:middle], own[middle:]), (oth[:middle], oth[middle:])


def attention_kernel(start, query, kv0, kv1, key_at, residual, hidden, kv, *, heads, groups):
    rows = query.shape[0]
    split = kv0.shape[0]
    kv[:split, :] = kv0[...]
    kv[split:, :] = kv1[...]
    at = lax.rem(lax.broadcasted_iota(jnp.int32, (groups * rows, kv.shape[0]), 0), rows) + start[0]
    causal = at >= key_at[...]
    for head in range(heads):
        first = head * groups
        wanted = jnp.concatenate(
            [query[:, (first + g) * HD : (first + g + 1) * HD] for g in range(groups)], axis=0
        )
        scores = lax.dot_general(
            wanted,
            kv[:, head * HD : (head + 1) * HD],
            (((1,), (1,)), ((), ())),
            preferred_element_type=F32,
        ) / math.sqrt(HD)
        masked = jnp.where(causal, scores, -1e30)
        peak = jnp.max(masked, axis=1, keepdims=True)
        terms = jnp.where(causal, jnp.exp(masked - peak), 0.0)
        weights = (terms / jnp.sum(terms, axis=1, keepdims=True)).astype(BF)
        context = jnp.dot(
            weights,
            kv[:, (heads + head) * HD : (heads + head + 1) * HD],
            preferred_element_type=F32,
        )
        for g in range(groups):
            cols = slice((first + g) * HD, (first + g + 1) * HD)
            hidden[:, cols] = (
                residual[:, cols].astype(F32) + context[g * rows : (g + 1) * rows, :]
            ).astype(BF)


def attention(query, keys, values, residual, info):
    token_count, half_width = query.shape
    kv_width = keys.shape[1]
    steps = bits_of("tensor", 0)
    pieces = gather_pair(jnp.concatenate([keys, values], axis=1), steps)
    pieces = lax.optimization_barrier((*pieces, info))[:2]
    me = lax.axis_index("tensor")
    order = [0]
    for axis, mask in steps:
        order = order + [j ^ mask for j in order]
    source = me ^ jnp.array(order, jnp.int32)
    key_at = (source[:, None] * token_count + jnp.arange(token_count)[None, :]).reshape(1, -1)
    length = key_at.shape[1]
    groups = half_width // kv_width
    full = pl.BlockSpec(memory_space=pltpu.VMEM)
    return pl.pallas_call(
        functools.partial(attention_kernel, heads=kv_width // HD, groups=groups),
        in_specs=[pl.BlockSpec(memory_space=pltpu.SMEM)] + [full] * 5,
        out_specs=full,
        out_shape=jax.ShapeDtypeStruct((token_count, half_width), BF),
        scratch_shapes=[pltpu.VMEM((length, 2 * kv_width), BF)],
        cost_estimate=pl.CostEstimate(
            flops=4 * token_count * length * half_width,
            bytes_accessed=8 * token_count * half_width,
            transcendentals=token_count * length * half_width // HD,
        ),
        compiler_params=pltpu.CompilerParams(vmem_limit_bytes=16 << 20),
        name="attention",
    )((me * token_count)[None].astype(jnp.int32), query, *pieces, key_at, residual)


def on_device(query, keys, values, residual, routes, gates, w_gate, w_up, w_down):
    section = lax.axis_index("section")
    token_count, _ = query[0].shape
    share = token_count // 2
    experts = w_gate.shape[0]

    def rows_of(value, part):
        return lax.dynamic_slice_in_dim(value, part * share, share, 0)

    steps = gather_steps()
    info = jnp.concatenate([routes[0].astype(F32), gates[0]], axis=1)
    info = jnp.concatenate(gather_pair(rows_of(info, section), steps), axis=0)
    hidden = attention(query[0], keys[0], values[0], residual[0], info)
    sent = rows_of(hidden, 1 - section)
    came = named_swap(sent, ("section", 1))
    tokens = info.shape[0]
    ids = (lax.axis_index("expert") * experts + jnp.arange(experts)).astype(F32)
    order = jnp.arange(tokens)
    lines = info.T
    hits = lines[:TOP][None] == ids[:, None, None]
    match = jnp.any(hits, axis=1)
    gate_all = lines[TOP:]
    gate = jnp.sum(jnp.where(hits, gate_all[None], 0.0), axis=1)
    lower = (order[:, None] < order[None, :]).astype(BF)
    before = jnp.dot(match.astype(BF), lower, preferred_element_type=F32)
    rank = jnp.where(match, before, -1.0).astype(jnp.int32)
    match_t = jnp.any(info[:, :TOP][:, :, None] == ids[None, None, :], axis=1)
    upper = (order[:, None] > order[None, :]).astype(BF)
    before_t = jnp.dot(upper, match_t.astype(BF), preferred_element_type=F32)
    rank_t = jnp.where(match_t, before_t, -1.0).astype(jnp.int32)
    counts = jnp.sum(match, axis=1).astype(jnp.int32)
    scal = jnp.concatenate([section[None].astype(jnp.int32), counts])
    cap = tokens // share * min(CAP, share)
    main = min(cap, -(-tokens * TOP * 5 // (EXPERTS * 4)) // 16 * 16)

    table = (scal, rank, rank_t, gate)
    own, (scal, rank, rank_t, gate) = gather_four(rows_of(hidden, section), steps, table)
    oth, _ = gather_four(came, steps)
    if tokens <= 1024:
        partial = expert_inner(scal, own, rank, w_gate, w_up, None, main, cap)
        inner = expert_inner(scal, oth, rank, w_gate, w_up, partial, main, cap)
        pack = (scal, inner, rank, rank_t, gate, w_down)
        sum_oth = expert_outer(*pack, True, main, cap)
        sum_own = expert_outer(*pack, False, main, cap)
    else:
        x_own = jnp.concatenate(own, axis=0)
        x_oth = jnp.concatenate(oth, axis=0)
        sum_own, sum_oth = wide_experts(
            section, x_own, x_oth, rank, gate, w_gate, w_up, w_down, cap
        )
    sum_oth = scatter_sum(*sum_oth, steps)
    partner = named_swap(sum_oth, ("section", 1))
    sum_own = scatter_sum(*sum_own, steps)
    first = section == 0
    expert_sum = jnp.concatenate(
        [jnp.where(first, sum_own, partner), jnp.where(first, partner, sum_own)], axis=0
    )
    return (hidden.astype(F32) + expert_sum.astype(F32)).astype(BF)[None]


def solution(mesh):
    last = len([n for n in ("expert",) for _ in range(mesh.shape[n].bit_length() - 1)])
    last += mesh.shape["tensor"].bit_length() - 2
    return jax.shard_map(
        on_device,
        mesh=mesh,
        in_specs=(
            P("expert", "tensor", "section"),
            P("expert", "tensor", "section"),
            P("expert", "tensor", "section"),
            P("expert", "tensor", "section"),
            P("expert", "tensor", None),
            P("expert", "tensor", None),
            P("expert", None, "tensor"),
            P("expert", None, "tensor"),
            P("expert", "tensor", None),
        ),
        out_specs=P("expert", "tensor", "section"),
        check_vma=False,
    )
```

time: 205 us -> 171 us (0.83)
  Pallas kernels: 63.1 us -> 50.4 us
  local copies, waits for them, and re-layouts: 11.4 us -> 2.55 us
  waiting for transfers between devices: 87.1 us -> 79.8 us
  matrix products: 4.47 us -> 0.47 us
    pallas_call x2, Pallas kernels: 29.2 us -> 20.1 us  [expert_outer(): pl.pallas_call(functools.partial(outer_kernel, main=main, cap=cap), grid_...]
    ppermute x21 -> x27, waiting for transfers between devices: 87.1 us -> 79.8 us  [swap(): return lax.ppermute(value, axis, pairs)]
    pallas_call x1 -> x3, Pallas kernels: 34 us -> 30.3 us  [the longest x2 28.3 us: expert_inner(): pl.pallas_call(functools.partial(inner_kernel, main=main, cap=cap, split=...]
    slice x10 -> x8, local copies, waits for them, and re-layouts: 3.07 us -> 0.16 us  [the longest x6 0.15 us: scatter_sum(): total = add_rows(total[:half], named_swap(total[half:], steps[i]))]
    concatenate x3 -> x2, local copies, waits for them, and re-layouts: 2.57 us -> 0.11 us  [the longest x1 0.09 us: on_device(): info = jnp.concatenate(gather_pair(rows_of(info, section), steps), axis=0)]
    sub x1 -> x0, matrix products: 2.21 us -> none  [attention(): exp_terms = jnp.where(causal, jnp.exp(masked - row_peak), 0.0)]
    ppermute x21 -> x27, starting transfers between devices: 29.8 us -> 29.1 us  [swap(): return lax.ppermute(value, axis, pairs)]
  transfers between devices with their start and end apart: 21 -> 27, of which waited for: 14 -> 13; matrix products, arithmetic and copies ran while one was open for 5% -> 4% of each run, Pallas kernels for 7% -> 14%
where the time goes in v2:
time: 171 us; the launch traced here: 170 us
  waiting for transfers between devices  79.8 us (47%)
  Pallas kernels  50.4 us (29%)
  starting transfers between devices  29.1 us (17%)
  other arithmetic  7.57 us (4%)
  local copies, waits for them, and re-layouts  2.55 us (1%)
    ppermute x27, waiting for transfers between devices, swap(): return lax.ppermute(value, axis, pairs)  79.8 us
    ppermute x27, starting transfers between devices, swap(): return lax.ppermute(value, axis, pairs)  29.1 us
    pallas_call x2, Pallas kernels, expert_inner(): pl.pallas_call(functools.partial(inner_kernel, main=main, cap=cap, split=...  28.3 us
    pallas_call x2, Pallas kernels, expert_outer(): pl.pallas_call(functools.partial(outer_kernel, main=main, cap=cap), grid_...  20.1 us
  transfers between devices with their start and end apart: 27, of which 13 were waited for; matrix products, arithmetic and copies ran while one was open for 4% of the time, Pallas kernels for 14%

profile of v2, /device:TPU:0, one launch (start us, length us, event | category | flops | bytes accessed | tf_op | source)
XLA Modules:
  0.0 170.2 jit_solution(5477185997321087017)
XLA Ops:
  0.0 0.7 convert_bitcast_fusion
  0.7 0.7 pad_maximum_fusion.7
  1.4 0.1 constant_dynamic-slice_fusion.2
  1.4 4.1 %collective-permute-start.3 = (f32[32,4]{0,1:T(4,128)S(1)}, f32[32,4]{0,1:T(4,128)S(1)}, u32[]{:S(2)}, u32[]{:S(2)}) collective-permute-start(f32[32,4]{0,1:T(4,128)S(1)} %constant_dynamic-slice_fusion.2), channel_id=1, source_target_pairs={{0,4},{1,5},{2,6},{3,7},{4,0},{5,1},{6,2},{7,3},{8,12},{9,13},{10,... | collective-permute-start | bytes 1544 | tf_op jit(solution)/shard_map/ppermute | solution.py:22
  5.5 0.9 pad_maximum_fusion.5
  6.4 0.1 collective-permute-start
  6.5 0.7 xor_multiply_fusion
  7.2 1.9 %collective-permute-start.4 = (f32[64,4]{0,1:T(4,128)S(1)}, f32[64,4]{0,1:T(4,128)S(1)}, u32[]{:S(2)}, u32[]{:S(2)}) collective-permute-start(f32[64,4]{0,1:T(4,128)S(1)} %pad_maximum_fusion.8), channel_id=1, source_target_pairs={{0,2},{1,3},{2,0},{3,1},{4,6},{5,7},{6,4},{7,5},{8,10},{9,11},{10,... | collective-permute-start | bytes 3080 | tf_op jit(solution)/shard_map/ppermute | solution.py:22
  9.1 6.0 %collective-permute-done = bf16[64,1024]{1,0:T(8,128)(2,1)S(1)} collective-permute-done((bf16[64,1024]{1,0:T(8,128)(2,1)S(1)}, bf16[64,1024]{1,0:T(8,128)(2,1)S(1)}, u32[]{:S(2)}, u32[]{:S(2)}) %collective-permute-start) | collective-permute-done | bytes 131104 | tf_op jit(solution)/shard_map/ppermute | solution.py:22
  15.1 0.9 pad_maximum_fusion.2
  16.2 0.1 pad_maximum_fusion.9
  16.2 1.5 collective-permute-start.5
  17.7 5.6 %collective-permute-done.1 = bf16[128,1024]{1,0:T(8,128)(2,1)S(1)} collective-permute-done((bf16[128,1024]{1,0:T(8,128)(2,1)S(1)}, bf16[128,1024]{1,0:T(8,128)(2,1)S(1)}, u32[]{:S(2)}, u32[]{:S(2)}) %collective-permute-start.1) | collective-permute-done | bytes 262176 | tf_op jit(solution)/shard_map/ppermute | solution.py:22
  23.3 0.9 pad_maximum_fusion.kv0
  24.3 0.1 pad_maximum_fusion.6
  24.4 0.5 collective-permute-start.6
  24.9 0.1 add.75.key_at
  24.9 1.2 collective-permute-done.6
  26.2 0.1 concatenate.55
  26.3 0.1 compare_reduce_fusion.1
  26.4 0.9 copy-done
  27.4 0.9 copy-done.1
  28.3 2.0 %attention.1 = bf16[64,2048]{1,0:T(8,128)(2,1)S(1)} custom-call(s32[1]{0:T(128)} %bitcast.start, bf16[64,2048]{1,0:T(8,128)(2,1)S(1)} %bitcast.14, bf16[256,1024]{1,0:T(8,128)(2,1)S(1)} %pad_maximum_fusion.kv0, bf16[256,1024]{1,0:T(8,128)(2,1)S(1)} %collective-permute-done.2.kv1, s32[1,512]{1,0:T(1,128)S(1)} %add.75.key_at, bf16[64,2048]{1,0:T(8,128)(2,1)S(1)} %bitcast.15), custom_call_target="tpu_custom_call" | custom-call | flops 268435456 | bytes 1048576 | tf_op jit(solution)/shard_map/attention/pallas_call | solution.py:330
  30.4 1.2 collective-permute-start.7
  31.5 0.1 compare_reduce_fusion
  31.6 0.2 copy.13
  31.8 0.1 fusion.3.gate
  31.9 1.6 collective-permute-start.10
  33.5 5.9 %collective-permute-done.7 = bf16[32,2048]{1,0:T(8,128)(2,1)S(1)} collective-permute-done((bf16[32,2048]{1,0:T(8,128)(2,1)S(1)}, bf16[32,2048]{1,0:T(8,128)(2,1)S(1)}, u32[]{:S(2)}, u32[]{:S(2)}) %collective-permute-start.7) | collective-permute-done | bytes 131104 | tf_op jit(solution)/shard_map/ppermute | solution.py:22
  39.5 2.8 %collective-permute-start.11 = (bf16[32,2048]{1,0:T(8,128)(2,1)S(1)}, bf16[32,2048]{1,0:T(8,128)(2,1)S(1)}, u32[]{:S(2)}, u32[]{:S(2)}) collective-permute-start(bf16[32,2048]{1,0:T(8,128)(2,1)S(1)} %collective-permute-done.10), channel_id=1, source_target_pairs={{0,4},{1,5},{2,6},{3,7},{4,0},{5,1},{6,2},{7,3},{8,12},{9,13},{10,... | collective-permute-start | bytes 393224 | tf_op jit(solution)/shard_map/ppermute | solution.py:22
  42.4 6.0 %collective-permute-done.11 = bf16[32,2048]{1,0:T(8,128)(2,1)S(1)} collective-permute-done((bf16[32,2048]{1,0:T(8,128)(2,1)S(1)}, bf16[32,2048]{1,0:T(8,128)(2,1)S(1)}, u32[]{:S(2)}, u32[]{:S(2)}) %collective-permute-start.11) | collective-permute-done | bytes 131104 | tf_op jit(solution)/shard_map/ppermute | solution.py:22
  48.4 3.4 %collective-permute-start.12 = (bf16[64,2048]{1,0:T(8,128)(2,1)S(1)}, bf16[64,2048]{1,0:T(8,128)(2,1)S(1)}, u32[]{:S(2)}, u32[]{:S(2)}) collective-permute-start(bf16[64,2048]{1,0:T(8,128)(2,1)S(1)} %pad_maximum_fusion.4), channel_id=1, source_target_pairs={{0,2},{1,3},{2,0},{3,1},{4,6},{5,7},{6,4},{7,5},{8,10},{9,11},{10,... | collective-permute-start | bytes 786440 | tf_op jit(solution)/shard_map/ppermute | solution.py:22
  51.8 1.6 collective-permute-start.16
  53.4 4.3 %collective-permute-done.12 = bf16[64,2048]{1,0:T(8,128)(2,1)S(1)} collective-permute-done((bf16[64,2048]{1,0:T(8,128)(2,1)S(1)}, bf16[64,2048]{1,0:T(8,128)(2,1)S(1)}, u32[]{:S(2)}, u32[]{:S(2)}) %collective-permute-start.12) | collective-permute-done | bytes 262176 | tf_op jit(solution)/shard_map/ppermute | solution.py:22
  57.7 1.6 collective-permute-start.13
  59.3 0.1 convert_reduce_fusion
  59.5 7.2 %collective-permute-done.16.refs_1_ = bf16[128,2048]{1,0:T(8,128)(2,1)S(1)} collective-permute-done((bf16[128,2048]{1,0:T(8,128)(2,1)S(1)}, bf16[128,2048]{1,0:T(8,128)(2,1)S(1)}, u32[]{:S(2)}, u32[]{:S(2)}) %collective-permute-start.16) | collective-permute-done | bytes 524320 | tf_op jit(solution)/shard_map/ppermute | solution.py:22
  66.7 0.2 fusion.1.refs_4_.rank
  66.8 0.3 fusion.rank_t
  67.1 0.6 collective-permute-start.14
  67.7 8.4 %collective-permute-done.13.refs_1_ = bf16[128,2048]{1,0:T(8,128)(2,1)S(1)} collective-permute-done((bf16[128,2048]{1,0:T(8,128)(2,1)S(1)}, bf16[128,2048]{1,0:T(8,128)(2,1)S(1)}, u32[]{:S(2)}, u32[]{:S(2)}) %collective-permute-start.13) | collective-permute-done | bytes 524320 | tf_op jit(solution)/shard_map/ppermute | solution.py:22
  76.1 0.1 pad_add_fusion.scal
  76.2 14.1 %inner_first.1 = (f32[4,160,1024]{2,1,0:T(8,128)S(1)}, f32[4,160,1024]{2,1,0:T(8,128)S(1)}, f32[5,112,1024]{2,1,0:T(8,128)S(1)}, f32[5,112,1024]{2,1,0:T(8,128)S(1)}) custom-call(s32[5]{0:T(128)S(1)} %pad_add_fusion.scal, bf16[128,2048]{1,0:T(8,128)(2,1)S(1)} %pad_maximum_fusion.1.refs_0_, bf16[128,2048]{1,0:T(8,128)(2,1)S(1)} %collective-permute-done.16.refs_1_, ...), custom_call_target="tpu_custom_call" | custom-call | flops 5368709120 | bytes 33554432 | tf_op jit(solution)/shard_map/inner_first/pallas_call | solution.py:142
  90.3 14.1 %inner_last.1.inner = bf16[4,272,1024]{2,1,0:T(8,128)(2,1)S(1)} custom-call(s32[5]{0:T(128)S(1)} %pad_add_fusion.scal, bf16[128,2048]{1,0:T(8,128)(2,1)S(1)} %constant_dynamic-update-slice_fusion.refs_0_, bf16[128,2048]{1,0:T(8,128)(2,1)S(1)} %collective-permute-done.13.refs_1_, bf16[128,2048]{1,0:T(8,128)(2,1)S(1)} %collective-permute-done.14.refs_2_, ...), custom_call_target="tpu_custom_call" | custom-call | flops 5368709120 | bytes 33554432 | tf_op jit(solution)/shard_map/inner_last/pallas_call | solution.py:142
  104.5 9.9 %outer_other.1 = (bf16[256,2048]{1,0:T(8,128)(2,1)S(1)}, bf16[256,2048]{1,0:T(8,128)(2,1)S(1)}) custom-call(s32[5]{0:T(128)S(1)} %pad_add_fusion.scal, bf16[4,272,1024]{2,1,0:T(8,128)(2,1)S(1)} %inner_last.1.inner, s32[4,512]{1,0:T(4,128)S(1)} %fusion.1.refs_4_.rank, s32[512,4]{1,0:T(8,128)S(1)} %fusion.rank_t, f32[4,512]{1,0:T(4,128)S(1)} %fusion.3.gate, ...), custom_call_target="tpu_custom_call" | custom-call | flops 4026531840 | bytes 16777216 | tf_op jit(solution)/shard_map/outer_other/pallas_call | solution.py:224
  114.4 0.6 collective-permute-start.22
  115.0 10.1 %outer_own.1 = (bf16[256,2048]{1,0:T(8,128)(2,1)S(1)}, bf16[256,2048]{1,0:T(8,128)(2,1)S(1)}) custom-call(s32[5]{0:T(128)S(1)} %pad_add_fusion.scal, bf16[4,272,1024]{2,1,0:T(8,128)(2,1)S(1)} %inner_last.1.inner, s32[4,512]{1,0:T(4,128)S(1)} %fusion.1.refs_4_.rank, s32[512,4]{1,0:T(8,128)S(1)} %fusion.rank_t, f32[4,512]{1,0:T(4,128)S(1)} %fusion.3.gate, ...), custom_call_target="tpu_custom_call" | custom-call | flops 4026531840 | bytes 16777216 | tf_op jit(solution)/shard_map/outer_own/pallas_call | solution.py:224
  125.1 0.1 collective-permute-start.18
  125.2 0.4 add_convert_fusion
  125.7 1.6 collective-permute-start.23
  127.3 0.6 collective-permute-done.18
  127.9 0.4 add_convert_fusion.1
  128.3 1.6 collective-permute-start.19
  129.9 10.6 %collective-permute-done.23 = bf16[128,2048]{1,0:T(8,128)(2,1)S(1)} collective-permute-done((bf16[128,2048]{1,0:T(8,128)(2,1)S(1)}, bf16[128,2048]{1,0:T(8,128)(2,1)S(1)}, u32[]{:S(2)}, u32[]{:S(2)}) %collective-permute-start.23) | collective-permute-done | bytes 524320 | tf_op jit(solution)/shard_map/ppermute | solution.py:22
  140.6 0.1 add_convert_fusion.2
  140.7 0.4 collective-permute-start.24
  141.1 10.2 %collective-permute-done.19 = bf16[128,2048]{1,0:T(8,128)(2,1)S(1)} collective-permute-done((bf16[128,2048]{1,0:T(8,128)(2,1)S(1)}, bf16[128,2048]{1,0:T(8,128)(2,1)S(1)}, u32[]{:S(2)}, u32[]{:S(2)}) %collective-permute-start.19) | collective-permute-done | bytes 524320 | tf_op jit(solution)/shard_map/ppermute | solution.py:22
  151.3 0.1 add_convert_fusion.3
  151.5 0.4 collective-permute-start.20
  151.9 1.9 %collective-permute-start.25 = (bf16[32,2048]{1,0:T(8,128)(2,1)S(1)}, bf16[32,2048]{1,0:T(8,128)(2,1)S(1)}, u32[]{:S(2)}, u32[]{:S(2)}) collective-permute-start(bf16[32,2048]{1,0:T(8,128)(2,1)S(1)} %slice.74), channel_id=1, source_target_pairs={{0,4},{1,5},{2,6},{3,7},{4,0},{5,1},{6,2},{7,3},{8,12},{9,13},{10,... | collective-permute-start | bytes 393224 | tf_op jit(solution)/shard_map/ppermute | solution.py:22
  153.8 8.4 %collective-permute-done.20 = bf16[64,2048]{1,0:T(8,128)(2,1)S(1)} collective-permute-done((bf16[64,2048]{1,0:T(8,128)(2,1)S(1)}, bf16[64,2048]{1,0:T(8,128)(2,1)S(1)}, u32[]{:S(2)}, u32[]{:S(2)}) %collective-permute-start.20) | collective-permute-done | bytes 262176 | tf_op jit(solution)/shard_map/ppermute | solution.py:22
  162.4 1.6 collective-permute-start.26
  164.0 5.3 %collective-permute-done.21 = bf16[32,2048]{1,0:T(8,128)(2,1)S(1)} collective-permute-done((bf16[32,2048]{1,0:T(8,128)(2,1)S(1)}, bf16[32,2048]{1,0:T(8,128)(2,1)S(1)}, u32[]{:S(2)}, u32[]{:S(2)}) %collective-permute-start.21) | collective-permute-done | bytes 131104 | tf_op jit(solution)/shard_map/ppermute | solution.py:22
  169.4 0.8 fusion.2
  (45 shorter events, 1.1 us)
Async XLA Ops:
  1.4 5.7 %collective-permute-start.3 = (f32[32,4]{0,1:T(4,128)S(1)}, f32[32,4]{0,1:T(4,128)S(1)}, u32[]{:S(2)}, u32[]{:S(2)}) collective-permute-start(f32[32,4]{0,1:T(4,128)S(1)} %constant_dynamic-slice_fusion.2), channel_id=1, source_target_pairs={{0,4},{1,5},{2,6},{3,7},{4,0},{5,1},{6,2},{7,3},{8,12},{9,13},{10,... | collective-permute-start | bytes 1544 | tf_op jit(solution)/shard_map/ppermute | solution.py:22
  6.4 8.7 %collective-permute-start = (bf16[64,1024]{1,0:T(8,128)(2,1)S(1)}, bf16[64,1024]{1,0:T(8,128)(2,1)S(1)}, u32[]{:S(2)}, u32[]{:S(2)}) collective-permute-start(bf16[64,1024]{1,0:T(8,128)(2,1)S(1)} %pad_maximum_fusion.5), channel_id=1, source_target_pairs={{0,4},{1,5},{2,6},{3,7},{4,0},{5,1},{6,2},{7,3},{8,12},{9,13},{10,... | collective-permute-start | bytes 393224 | tf_op jit(solution)/shard_map/ppermute | solution.py:22
  7.2 9.0 %collective-permute-start.4 = (f32[64,4]{0,1:T(4,128)S(1)}, f32[64,4]{0,1:T(4,128)S(1)}, u32[]{:S(2)}, u32[]{:S(2)}) collective-permute-start(f32[64,4]{0,1:T(4,128)S(1)} %pad_maximum_fusion.8), channel_id=1, source_target_pairs={{0,2},{1,3},{2,0},{3,1},{4,6},{5,7},{6,4},{7,5},{8,10},{9,11},{10,... | collective-permute-start | bytes 3080 | tf_op jit(solution)/shard_map/ppermute | solution.py:22
  16.0 7.3 %collective-permute-start.1 = (bf16[128,1024]{1,0:T(8,128)(2,1)S(1)}, bf16[128,1024]{1,0:T(8,128)(2,1)S(1)}, u32[]{:S(2)}, u32[]{:S(2)}) collective-permute-start(bf16[128,1024]{1,0:T(8,128)(2,1)S(1)} %pad_maximum_fusion.2), channel_id=1, source_target_pairs={{0,2},{1,3},{2,0},{3,1},{4,6},{5,7},{6,4},{7,5},{8,10},{9,11},{10,... | collective-permute-start | bytes 786440 | tf_op jit(solution)/shard_map/ppermute | solution.py:22
  16.2 8.0 %collective-permute-start.5 = (f32[128,4]{0,1:T(4,128)S(1)}, f32[128,4]{0,1:T(4,128)S(1)}, u32[]{:S(2)}, u32[]{:S(2)}) collective-permute-start(f32[128,4]{0,1:T(4,128)S(1)} %pad_maximum_fusion.9), channel_id=1, source_target_pairs={{0,8},{8,0},{1,9},{9,1},{2,10},{10,2},{3,11},{11,3},{4,12},{12,4},... | collective-permute-start | bytes 6152 | tf_op jit(solution)/shard_map/ppermute | solution.py:22
  24.2 2.2 %collective-permute-start.2 = (bf16[256,1024]{1,0:T(8,128)(2,1)S(1)}, bf16[256,1024]{1,0:T(8,128)(2,1)S(1)}, u32[]{:S(2)}, u32[]{:S(2)}) collective-permute-start(bf16[256,1024]{1,0:T(8,128)(2,1)S(1)} %pad_maximum_fusion.kv0), channel_id=1, source_target_pairs={{0,1},{1,0},{2,3},{3,2},{4,5},{5,4},{6,7},{7,6},{8,9},{9,8},{10,11... | collective-permute-start | bytes 1572872 | tf_op jit(solution)/shard_map/ppermute | solution.py:22
  24.4 1.8 %collective-permute-start.6 = (f32[256,4]{0,1:T(4,128)S(1)}, f32[256,4]{0,1:T(4,128)S(1)}, u32[]{:S(2)}, u32[]{:S(2)}) collective-permute-start(f32[256,4]{0,1:T(4,128)S(1)} %pad_maximum_fusion.6), channel_id=1, source_target_pairs={{0,1},{1,0},{2,3},{3,2},{4,5},{5,4},{6,7},{7,6},{8,9},{9,8},{10,11... | collective-permute-start | bytes 12296 | tf_op jit(solution)/shard_map/ppermute | solution.py:22
  26.4 1.0 copy-start
  27.4 0.9 copy-start.1
  30.4 9.0 %collective-permute-start.7 = (bf16[32,2048]{1,0:T(8,128)(2,1)S(1)}, bf16[32,2048]{1,0:T(8,128)(2,1)S(1)}, u32[]{:S(2)}, u32[]{:S(2)}) collective-permute-start(bf16[32,2048]{1,0:T(8,128)(2,1)S(1)} %get-tuple-element.38), channel_id=1, source_target_pairs={{0,4},{1,5},{2,6},{3,7},{4,0},{5,1},{6,2},{7,3},{8,12},{9,13},{10,... | collective-permute-start | bytes 393224 | tf_op jit(solution)/shard_map/ppermute | solution.py:22
  31.9 7.6 %collective-permute-start.10 = (bf16[32,2048]{1,0:T(8,128)(2,1)S(1)}, bf16[32,2048]{1,0:T(8,128)(2,1)S(1)}, u32[]{:S(2)}, u32[]{:S(2)}) collective-permute-start(bf16[32,2048]{1,0:T(8,128)(2,1)S(1)} %get-tuple-element.37), channel_id=1, source_target_pairs={{0,16},{16,0},{1,17},{17,1},{2,18},{18,2},{3,19},{19,3},{4,20},{20... | collective-permute-start | bytes 393224 | tf_op jit(solution)/shard_map/ppermute | solution.py:22
  39.4 12.3 %collective-permute-start.8 = (bf16[64,2048]{1,0:T(8,128)(2,1)S(1)}, bf16[64,2048]{1,0:T(8,128)(2,1)S(1)}, u32[]{:S(2)}, u32[]{:S(2)}) collective-permute-start(bf16[64,2048]{1,0:T(8,128)(2,1)S(1)} %pad_maximum_fusion.3), channel_id=1, source_target_pairs={{0,2},{1,3},{2,0},{3,1},{4,6},{5,7},{6,4},{7,5},{8,10},{9,11},{10,... | collective-permute-start | bytes 786440 | tf_op jit(solution)/shard_map/ppermute | solution.py:22
  39.5 8.8 %collective-permute-start.11 = (bf16[32,2048]{1,0:T(8,128)(2,1)S(1)}, bf16[32,2048]{1,0:T(8,128)(2,1)S(1)}, u32[]{:S(2)}, u32[]{:S(2)}) collective-permute-start(bf16[32,2048]{1,0:T(8,128)(2,1)S(1)} %collective-permute-done.10), channel_id=1, source_target_pairs={{0,4},{1,5},{2,6},{3,7},{4,0},{5,1},{6,2},{7,3},{8,12},{9,13},{10,... | collective-permute-start | bytes 393224 | tf_op jit(solution)/shard_map/ppermute | solution.py:22
  48.4 9.3 %collective-permute-start.12 = (bf16[64,2048]{1,0:T(8,128)(2,1)S(1)}, bf16[64,2048]{1,0:T(8,128)(2,1)S(1)}, u32[]{:S(2)}, u32[]{:S(2)}) collective-permute-start(bf16[64,2048]{1,0:T(8,128)(2,1)S(1)} %pad_maximum_fusion.4), channel_id=1, source_target_pairs={{0,2},{1,3},{2,0},{3,1},{4,6},{5,7},{6,4},{7,5},{8,10},{9,11},{10,... | collective-permute-start | bytes 786440 | tf_op jit(solution)/shard_map/ppermute | solution.py:22
  51.8 14.9 %collective-permute-start.16 = (bf16[128,2048]{1,0:T(8,128)(2,1)S(1)}, bf16[128,2048]{1,0:T(8,128)(2,1)S(1)}, u32[]{:S(2)}, u32[]{:S(2)}) collective-permute-start(bf16[128,2048]{1,0:T(8,128)(2,1)S(1)} %pad_maximum_fusion.1.refs_0_), channel_id=1, source_target_pairs={{0,8},{8,0},{1,9},{9,1},{2,10},{10,2},{3,11},{11,3},{4,12},{12,4},... | collective-permute-start | bytes 1572872 | tf_op jit(solution)/shard_map/ppermute | solution.py:22
  57.7 18.4 %collective-permute-start.13 = (bf16[128,2048]{1,0:T(8,128)(2,1)S(1)}, bf16[128,2048]{1,0:T(8,128)(2,1)S(1)}, u32[]{:S(2)}, u32[]{:S(2)}) collective-permute-start(bf16[128,2048]{1,0:T(8,128)(2,1)S(1)} %constant_dynamic-update-slice_fusion.refs_0_), channel_id=1, source_target_pairs={{0,8},{8,0},{1,9},{9,1},{2,10},{10,2},{3,11},{11,3},{4,12},{12,4},... | collective-permute-start | bytes 1572872 | tf_op jit(solution)/shard_map/ppermute | solution.py:22
  59.4 16.8 %collective-permute-start.9 = (bf16[128,2048]{1,0:T(8,128)(2,1)S(1)}, bf16[128,2048]{1,0:T(8,128)(2,1)S(1)}, u32[]{:S(2)}, u32[]{:S(2)}) collective-permute-start(bf16[128,2048]{1,0:T(8,128)(2,1)S(1)} %pad_maximum_fusion.1.refs_0_), channel_id=1, source_target_pairs={{0,1},{1,0},{2,3},{3,2},{4,5},{5,4},{6,7},{7,6},{8,9},{9,8},{10,11... | collective-permute-start | bytes 1572872 | tf_op jit(solution)/shard_map/ppermute | solution.py:22
  66.7 9.5 %collective-permute-start.17 = (bf16[128,2048]{1,0:T(8,128)(2,1)S(1)}, bf16[128,2048]{1,0:T(8,128)(2,1)S(1)}, u32[]{:S(2)}, u32[]{:S(2)}) collective-permute-start(bf16[128,2048]{1,0:T(8,128)(2,1)S(1)} %collective-permute-done.16.refs_1_), channel_id=1, source_target_pairs={{0,1},{1,0},{2,3},{3,2},{4,5},{5,4},{6,7},{7,6},{8,9},{9,8},{10,11... | collective-permute-start | bytes 1572872 | tf_op jit(solution)/shard_map/ppermute | solution.py:22
  67.1 23.2 %collective-permute-start.14 = (bf16[128,2048]{1,0:T(8,128)(2,1)S(1)}, bf16[128,2048]{1,0:T(8,128)(2,1)S(1)}, u32[]{:S(2)}, u32[]{:S(2)}) collective-permute-start(bf16[128,2048]{1,0:T(8,128)(2,1)S(1)} %constant_dynamic-update-slice_fusion.refs_0_), channel_id=1, source_target_pairs={{0,1},{1,0},{2,3},{3,2},{4,5},{5,4},{6,7},{7,6},{8,9},{9,8},{10,11... | collective-permute-start | bytes 1572872 | tf_op jit(solution)/shard_map/ppermute | solution.py:22
  76.1 14.2 %collective-permute-start.15 = (bf16[128,2048]{1,0:T(8,128)(2,1)S(1)}, bf16[128,2048]{1,0:T(8,128)(2,1)S(1)}, u32[]{:S(2)}, u32[]{:S(2)}) collective-permute-start(bf16[128,2048]{1,0:T(8,128)(2,1)S(1)} %collective-permute-done.13.refs_1_), channel_id=1, source_target_pairs={{0,1},{1,0},{2,3},{3,2},{4,5},{5,4},{6,7},{7,6},{8,9},{9,8},{10,11... | collective-permute-start | bytes 1572872 | tf_op jit(solution)/shard_map/ppermute | solution.py:22
  114.4 10.8 %collective-permute-start.22 = (bf16[256,2048]{1,0:T(8,128)(2,1)S(1)}, bf16[256,2048]{1,0:T(8,128)(2,1)S(1)}, u32[]{:S(2)}, u32[]{:S(2)}) collective-permute-start(bf16[256,2048]{1,0:T(8,128)(2,1)S(1)} %get-tuple-element.34), channel_id=1, source_target_pairs={{0,1},{1,0},{2,3},{3,2},{4,5},{5,4},{6,7},{7,6},{8,9},{9,8},{10,11... | collective-permute-start | bytes 3145736 | tf_op jit(solution)/shard_map/ppermute | solution.py:22
  125.1 2.7 %collective-permute-start.18 = (bf16[256,2048]{1,0:T(8,128)(2,1)S(1)}, bf16[256,2048]{1,0:T(8,128)(2,1)S(1)}, u32[]{:S(2)}, u32[]{:S(2)}) collective-permute-start(bf16[256,2048]{1,0:T(8,128)(2,1)S(1)} %get-tuple-element.32), channel_id=1, source_target_pairs={{0,1},{1,0},{2,3},{3,2},{4,5},{5,4},{6,7},{7,6},{8,9},{9,8},{10,11... | collective-permute-start | bytes 3145736 | tf_op jit(solution)/shard_map/ppermute | solution.py:22
  125.7 14.9 %collective-permute-start.23 = (bf16[128,2048]{1,0:T(8,128)(2,1)S(1)}, bf16[128,2048]{1,0:T(8,128)(2,1)S(1)}, u32[]{:S(2)}, u32[]{:S(2)}) collective-permute-start(bf16[128,2048]{1,0:T(8,128)(2,1)S(1)} %slice.70), channel_id=1, source_target_pairs={{0,8},{8,0},{1,9},{9,1},{2,10},{10,2},{3,11},{11,3},{4,12},{12,4},... | collective-permute-start | bytes 1572872 | tf_op jit(solution)/shard_map/ppermute | solution.py:22
  128.3 23.0 %collective-permute-start.19 = (bf16[128,2048]{1,0:T(8,128)(2,1)S(1)}, bf16[128,2048]{1,0:T(8,128)(2,1)S(1)}, u32[]{:S(2)}, u32[]{:S(2)}) collective-permute-start(bf16[128,2048]{1,0:T(8,128)(2,1)S(1)} %slice.64), channel_id=1, source_target_pairs={{0,8},{8,0},{1,9},{9,1},{2,10},{10,2},{3,11},{11,3},{4,12},{12,4},... | collective-permute-start | bytes 1572872 | tf_op jit(solution)/shard_map/ppermute | solution.py:22
  140.7 11.1 %collective-permute-start.24 = (bf16[64,2048]{1,0:T(8,128)(2,1)S(1)}, bf16[64,2048]{1,0:T(8,128)(2,1)S(1)}, u32[]{:S(2)}, u32[]{:S(2)}) collective-permute-start(bf16[64,2048]{1,0:T(8,128)(2,1)S(1)} %slice.72), channel_id=1, source_target_pairs={{0,2},{1,3},{2,0},{3,1},{4,6},{5,7},{6,4},{7,5},{8,10},{9,11},{10,... | collective-permute-start | bytes 786440 | tf_op jit(solution)/shard_map/ppermute | solution.py:22
  151.5 10.7 %collective-permute-start.20 = (bf16[64,2048]{1,0:T(8,128)(2,1)S(1)}, bf16[64,2048]{1,0:T(8,128)(2,1)S(1)}, u32[]{:S(2)}, u32[]{:S(2)}) collective-permute-start(bf16[64,2048]{1,0:T(8,128)(2,1)S(1)} %slice.66), channel_id=1, source_target_pairs={{0,2},{1,3},{2,0},{3,1},{4,6},{5,7},{6,4},{7,5},{8,10},{9,11},{10,... | collective-permute-start | bytes 786440 | tf_op jit(solution)/shard_map/ppermute | solution.py:22
  151.9 10.4 %collective-permute-start.25 = (bf16[32,2048]{1,0:T(8,128)(2,1)S(1)}, bf16[32,2048]{1,0:T(8,128)(2,1)S(1)}, u32[]{:S(2)}, u32[]{:S(2)}) collective-permute-start(bf16[32,2048]{1,0:T(8,128)(2,1)S(1)} %slice.74), channel_id=1, source_target_pairs={{0,4},{1,5},{2,6},{3,7},{4,0},{5,1},{6,2},{7,3},{8,12},{9,13},{10,... | collective-permute-start | bytes 393224 | tf_op jit(solution)/shard_map/ppermute | solution.py:22
  162.3 7.1 %collective-permute-start.21 = (bf16[32,2048]{1,0:T(8,128)(2,1)S(1)}, bf16[32,2048]{1,0:T(8,128)(2,1)S(1)}, u32[]{:S(2)}, u32[]{:S(2)}) collective-permute-start(bf16[32,2048]{1,0:T(8,128)(2,1)S(1)} %slice.68), channel_id=1, source_target_pairs={{0,4},{1,5},{2,6},{3,7},{4,0},{5,1},{6,2},{7,3},{8,12},{9,13},{10,... | collective-permute-start | bytes 393224 | tf_op jit(solution)/shard_map/ppermute | solution.py:22
  162.4 7.0 %collective-permute-start.26 = (bf16[32,2048]{1,0:T(8,128)(2,1)S(1)}, bf16[32,2048]{1,0:T(8,128)(2,1)S(1)}, u32[]{:S(2)}, u32[]{:S(2)}) collective-permute-start(bf16[32,2048]{1,0:T(8,128)(2,1)S(1)} %add_convert_fusion.7), channel_id=1, source_target_pairs={{0,16},{16,0},{1,17},{17,1},{2,18},{18,2},{3,19},{19,3},{4,20},{20... | collective-permute-start | bytes 393224 | tf_op jit(solution)/shard_map/ppermute | solution.py:22
